TPU v7x, 32 devices: a whole 2x2x4 slice. The times are simulated.
32 devices in a mesh: region: 4 (over z), depth: 2 (over y), member: 4 (over x, core).
Axes of the slice: x: 2, y: 2, z: 4, core: 2. Of those that a mesh axis runs over, the one named last changes fastest.
Arguments:
- ensemble: bfloat16 [14, 384, 4096], P('depth', 'member', 'region'), may hold values from -6 to 6
- obs_weights: float32 [14], P('depth'), may hold values from -1.5 to 1.5
- obs_tiles: int32 [2048], P('region'), may hold values from 0 to 1023
- obs_values: float32 [2048], P('region'), may hold values from -8 to 8
- obs_error: float32 [2048], P('region'), may hold values from 0.2 to 2
- obs_noise: float32 [384, 2048], P('member', 'region'), may hold values from -6 to 6
Outputs:
- analysis: bfloat16 [14, 384, 4096], P('depth', 'member', 'region')
- inflation: float32 [], replicated
Inputs may be any that keep to these rules, and one draw needn't show every extreme that they name: `obs_tiles`: the tile of the observation, counted within the 1024 tiles of the region whose block holds the observation.
All inputs are finite; a program needn't handle non-finite values.
Results may differ from a plain program's by a relative error of at most 0.011.
Values may be sent and summed in bfloat16 or wider, within the bound.
A program may use at most 64 MiB of HBM per device.

v0:
```python
import functools

import jax
import jax.numpy as jnp
from jax import lax
from jax.experimental import pallas as pl
from jax.experimental.pallas import tpu as pltpu
from jax.sharding import PartitionSpec as P

RADIUS = 1024
EARLY = 2
F32 = jnp.float32
BF16 = jnp.bfloat16
MESH = pl.DeviceIdType.MESH


def kernel(
    sizes,
    weights,
    ensemble,
    tiles,
    values,
    errors,
    noise,
    out,
    infl_out,
    own,
    gathered,
    noise_v,
    part,
    part_in,
    squares,
    totals,
    stats,
    obs,
    pert,
    obs_t,
    taper,
    anom,
    means,
    gain,
    result,
    local_sem,
    send_e,
    recv_e,
    send_p,
    recv_p,
    send_q,
    recv_q,
    send_o,
    recv_o,
    send_g,
    recv_g,
    send_z,
    recv_z,
    send_st,
    recv_st,
    send_ps,
    recv_ps,
    send_pz,
    recv_pz,
    send_pf,
    recv_pf,
    send_f,
    recv_f,
    send_out,
    recv_out,
    own_out,
):
    nr, nd, nm, nl, mm, tt, kk = sizes
    ng = nm // 2
    half = tt // 2
    members = nm * mm
    r = lax.axis_index("region")
    d = lax.axis_index("depth")
    me = lax.axis_index("member")
    q = me // 2
    c = me % 2
    sib = 2 * q + (1 - c)
    has_side = (r > 0, r < nr - 1)

    def dev(region=None, depth=None, member=None):
        return {
            "region": r if region is None else region,
            "depth": d if depth is None else depth,
            "member": me if member is None else member,
        }

    def rdma(src, dst, ssem, rsem, device):
        return pltpu.make_async_remote_copy(
            src_ref=src,
            dst_ref=dst,
            send_sem=ssem,
            recv_sem=rsem,
            device_id=device,
            device_id_type=MESH,
        )

    local_own = pltpu.make_async_copy(ensemble, own, local_sem.at[0])
    local_own.start()
    local_half = pltpu.make_async_copy(
        ensemble.at[:, :, pl.ds(pl.multiple_of(c * half, 128), half)],
        gathered.at[:, me],
        local_sem.at[1],
    )
    local_half.start()
    local_noise = pltpu.make_async_copy(noise, noise_v, local_sem.at[2])
    local_noise.start()

    group = [(i, 0) for i in range(1, nd)] + [(0, j) for j in range(1, nm)]
    barrier = pltpu.get_barrier_semaphore()
    signals = 0
    for i, j in group:
        pl.semaphore_signal(
            barrier,
            inc=1,
            device_id=dev(depth=(d + i) % nd, member=(me + j) % nm),
            device_id_type=MESH,
        )
        signals += 1
    for i in range(1, nr):
        pl.semaphore_signal(
            barrier, inc=1, device_id=dev(region=(r + i) % nr), device_id_type=MESH
        )
        signals += 1
    pl.semaphore_wait(barrier, signals)

    def bulk(l, j):
        to = (me + j) % nm
        return rdma(
            ensemble.at[l, :, pl.ds(pl.multiple_of((to % 2) * half, 128), half)],
            gathered.at[l, me],
            send_e.at[l, j],
            recv_e.at[l, me],
            dev(member=to),
        )

    def send_bulk(l):
        for j in range(1, nm):
            bulk(l, j).start()

    send_bulk(0)
    local_own.wait()
    total = own[0].astype(F32) * weights[0]
    for l in range(1, nl):
        total = total + own[l].astype(F32) * weights[l]
    hi = total.astype(BF16)
    rest = total - hi.astype(F32)
    mid = rest.astype(BF16)
    low = (rest - mid.astype(F32)).astype(BF16)
    tile_ids = lax.broadcasted_iota(jnp.int32, (tt, kk), 0)
    onehot = jnp.where(tile_ids == tiles[...], 1.0, 0.0).astype(BF16)
    picked = (
        jnp.dot(hi, onehot, preferred_element_type=F32)
        + jnp.dot(mid, onehot, preferred_element_type=F32)
        + jnp.dot(low, onehot, preferred_element_type=F32)
    )
    part_mean = jnp.sum(picked, axis=0, keepdims=True) / mm
    top = part_mean.astype(BF16).astype(F32)
    second_row = (part_mean - top).astype(BF16).astype(F32)
    third_row = part_mean - top - second_row
    prow = lax.broadcasted_iota(jnp.int32, (16, kk), 0)
    split = jnp.where(prow == 0, top, jnp.where(prow == 1, second_row, third_row))
    part[0:mm] = (picked - part_mean).astype(BF16)
    part[mm : mm + 16] = jnp.where(prow < 3, split, 0.0).astype(BF16)

    def whole(block):
        values_of = block.astype(F32)
        return values_of[0:mm] + jnp.sum(values_of[mm : mm + 16], axis=0, keepdims=True)

    def part_copy(i):
        to = (d + i) % nd
        return rdma(part, part_in.at[d], send_p.at[i], recv_p.at[d], dev(depth=to))

    def part_from(i):
        frm = (d + i) % nd
        return rdma(part, part_in.at[frm], send_p.at[i], recv_p.at[frm], dev(depth=frm))

    for i in range(1, nd):
        part_copy(i).start()

    predicted = whole(part[...])
    for i in range(1, nd):
        part_from(i).wait_recv()
        predicted = predicted + whole(part_in[(d + i) % nd])
    own_sum = jnp.sum(predicted, axis=0, keepdims=True)
    spread_in = predicted - own_sum / mm
    own_square = jnp.sum(spread_in * spread_in, axis=0, keepdims=True)
    krow = lax.broadcasted_iota(jnp.int32, (8, kk), 0)
    squares[me] = jnp.where(krow == 0, own_sum, own_square)
    obs[me, :, kk : 2 * kk] = spread_in.astype(BF16)

    def square_copy(j, slot):
        return rdma(
            squares.at[slot],
            squares.at[slot],
            send_q.at[j],
            recv_q.at[slot],
            dev(member=(me + j) % nm),
        )

    def obs_copy(j, slot):
        block = obs.at[slot, :, pl.ds(kk, kk)]
        return rdma(block, block, send_o.at[j], recv_o.at[slot], dev(member=(me + j) % nm))

    def side_obs(side, slot, pair):
        window = 2 * kk if side == 0 else 0
        return rdma(
            obs.at[slot, :, pl.ds(kk, kk)],
            obs.at[slot, :, pl.ds(window, kk)],
            send_z.at[side, pair],
            recv_z.at[1 - side, pair],
            dev(region=r + (2 * side - 1)),
        )

    def obs_forward(w, slot, pair):
        block = obs.at[slot, :, pl.ds(w * kk, kk)]
        return rdma(block, block, send_f.at[w, pair], recv_f.at[w, pair], dev(member=sib))

    def cross(g):
        return 2 * ((q + g) % ng) + c

    def cross_sib(g):
        return 2 * ((q + g) % ng) + (1 - c)

    for j in range(1, nm):
        square_copy(j, me).start()
    for g in range(1, ng):
        obs_copy(2 * g, me).start()
    obs_forward(1, me, 0).start()
    for side in (0, 1):

        @pl.when(has_side[side])
        def _():
            side_obs(side, me, 0).start()

        @pl.when(jnp.logical_not(has_side[side]))
        def _():
            window = 0 if side == 0 else 2 * kk
            obs[:, :, window : window + kk] = jnp.zeros((nm, mm, kk), BF16)
            pert[:, :, window : window + kk] = jnp.zeros((2, mm, kk), BF16)
            stats[2 * side] = jnp.zeros((8, kk), F32)

    def send_rest(l, carry):
        send_bulk(l)
        return carry

    lax.fori_loop(1, nl, send_rest, 0)

    for j in range(1, nm):
        square_copy(j, (me + j) % nm).wait_recv()
    moments = [squares[j] for j in range(nm)]
    obs_mean = sum(m[0:1] for m in moments) / members
    deviation = predicted - obs_mean
    square_sum = sum(
        m[1:2] + mm * (m[0:1] / mm - obs_mean) * (m[0:1] / mm - obs_mean) for m in moments
    )
    spread = square_sum / (members - 1)
    error = errors[...]
    innovation = values[...] - obs_mean
    first = jnp.sum(innovation * innovation, axis=1, keepdims=True)
    second = jnp.sum(spread + error, axis=1, keepdims=True)
    rows = lax.broadcasted_iota(jnp.int32, (8, 128), 0)
    totals[r] = jnp.where(rows == 0, first, second)

    def total_copy(i, slot):
        return rdma(
            totals.at[slot],
            totals.at[slot],
            send_g.at[i],
            recv_g.at[slot],
            dev(region=(r + i) % nr),
        )

    for i in range(1, nr):
        total_copy(i, r).start()

    for g in range(1, ng):
        obs_copy(2 * g, cross(g)).wait_recv()
        for side in (0, 1):

            @pl.when(has_side[side])
            def _():
                side_obs(side, cross(g), g).start()

        obs_forward(1, cross(g), g).start()

    for i in range(1, nr):
        total_copy(i, (r + i) % nr).wait_recv()
    grand = totals[0]
    for i in range(1, nr):
        grand = grand + totals[i]
    inflation = grand[0:1, 0:1] / grand[1:2, 0:1]
    root = jnp.sqrt(inflation)
    infl_out[...] = inflation
    factor = inflation / (inflation * spread + error)
    facts = jnp.where(krow == 0, tiles[...].astype(F32), factor / (members - 1))
    for g in range(nm):
        facts = jnp.where(krow == 2 + g, moments[g][0:1] / mm - obs_mean, facts)
    stats[1] = facts
    local_noise.wait()
    pert[c, :, kk : 2 * kk] = (
        innovation + jnp.sqrt(error) * noise_v[...] - root * deviation
    ).astype(BF16)

    def stat_copy(side):
        return rdma(
            stats.at[1],
            stats.at[2 - 2 * side],
            send_st.at[side],
            recv_st.at[1 - side],
            dev(region=r + (2 * side - 1)),
        )

    def sib_pert(slot):
        block = pert.at[slot, :, pl.ds(kk, kk)]
        return rdma(block, block, send_ps.at[0], recv_ps.at[0], dev(member=sib))

    def side_pert(side):
        window = 2 * kk if side == 0 else 0
        return rdma(
            pert.at[c, :, pl.ds(kk, kk)],
            pert.at[c, :, pl.ds(window, kk)],
            send_pz.at[side],
            recv_pz.at[1 - side],
            dev(region=r + (2 * side - 1)),
        )

    def pert_forward(side, slot):
        block = pert.at[slot, :, pl.ds(2 * kk * side, kk)]
        return rdma(block, block, send_pf.at[side], recv_pf.at[side], dev(member=sib))

    sib_pert(c).start()
    for side in (0, 1):

        @pl.when(has_side[side])
        def _():
            stat_copy(side).start()
            side_pert(side).start()

    lane = (lax.broadcasted_iota(jnp.int32, (kk, half), 1) + c * half).astype(F32)

    def make_taper(w):
        columns = stats[w].T
        position = columns[:, 0:1] + float((w - 1) * tt)
        close = jnp.maximum(0.0, 1.0 - jnp.abs(lane - position) * (1.0 / RADIUS))
        taper[w * kk : (w + 1) * kk] = close * close * columns[:, 1:2]

    def transpose_all(w):
        shifts = stats[w].T
        for g in range(nm):
            block = obs[g, :, w * kk : (w + 1) * kk].astype(F32).T + shifts[:, 2 + g : 3 + g]
            obs_t[w * kk : (w + 1) * kk, g * mm : (g + 1) * mm] = block.astype(BF16)

    step = kk // 2

    def gain_blocks(l, lo, hi):
        right = anom[l].reshape(members, half)

        def one_block(b, inner):
            at = (b + 2 * (b // 2)) if lo == 0 else b
            rows_of = pl.ds(pl.multiple_of(at * step, step), step)
            cov = jnp.dot(obs_t[rows_of], right, preferred_element_type=F32)
            gain[l, rows_of] = (cov * taper[rows_of]).astype(BF16)
            return inner

        lax.fori_loop(lo, hi, one_block, 0)

    def own_window(l, carry):
        for j in range(1, nm):
            slot = (me + j) % nm
            rdma(
                gathered.at[l, slot],
                gathered.at[l, slot],
                send_e.at[l, j],
                recv_e.at[l, slot],
                dev(member=slot),
            ).wait_recv()
        raw = gathered[l].astype(F32)
        mean = jnp.sum(jnp.sum(raw, axis=0), axis=0, keepdims=True) / members
        means[l] = jnp.broadcast_to(mean, (8, half))
        anom[l] = (raw - mean[None]).astype(BF16)
        gain_blocks(l, 2, 4)
        return carry

    make_taper(1)
    for g in range(ng):
        obs_forward(1, cross_sib(g), g).wait_recv()
    transpose_all(1)
    local_half.wait()
    early = min(EARLY, nl)
    own_window(0, 0)

    for g in range(ng):
        for side in (0, 1):

            @pl.when(has_side[side])
            def _():
                side_obs(1 - side, cross(g), g).wait_recv()
                obs_forward(2 * side, cross(g), g).start()

    for side in (0, 1):

        @pl.when(has_side[side])
        def _():
            rdma(
                stats.at[1],
                stats.at[2 * side],
                send_st.at[side],
                recv_st.at[side],
                dev(region=r + (2 * side - 1)),
            ).wait_recv()

        make_taper(2 * side)

    for side in (0, 1):

        @pl.when(has_side[side])
        def _():
            for g in range(ng):
                obs_forward(2 * side, cross_sib(g), g).wait_recv()

        transpose_all(2 * side)

    def out_half(l, which):
        return out.at[l, :, pl.ds(pl.multiple_of(which * half, 128), half)]

    def out_local(l):
        return pltpu.make_async_copy(result.at[l, c], out_half(l, c), own_out.at[l])

    def out_remote(l):
        return rdma(
            result.at[l, 1 - c], out_half(l, c), send_out.at[l], recv_out.at[l], dev(member=sib)
        )

    def out_from(l):
        return rdma(
            result.at[l, 1 - c], out_half(l, 1 - c), send_out.at[l], recv_out.at[l], dev(member=sib)
        )

    def one_variable(l, carry):
        @pl.when(l >= early)
        def _():
            own_window(l, 0)

        gain_blocks(l, 0, 4)

        @pl.when(l == 0)
        def _():
            for side in (0, 1):

                @pl.when(has_side[side])
                def _():
                    side_pert(1 - side).wait_recv()
                    pert_forward(side, c).start()

            for ahead in range(1, early):
                own_window(ahead, 0)
            sib_pert(1 - c).wait_recv()
            for side in (0, 1):

                @pl.when(has_side[side])
                def _():
                    pert_forward(side, 1 - c).wait_recv()

        increment = jnp.dot(
            pert[...].reshape(2 * mm, 3 * kk), gain[l], preferred_element_type=F32
        )
        base = means[l][0:1][None] + root[None] * anom[l, pl.ds(2 * q, 2)].astype(F32)
        result[l] = (base + increment.reshape(2, mm, half)).astype(BF16)
        out_local(l).start()
        out_remote(l).start()
        return carry

    lax.fori_loop(0, nl, one_variable, 0)

    def finish(l, carry):
        for j in range(1, nm):
            bulk(l, j).wait_send()
        out_local(l).wait()
        out_remote(l).wait_send()
        out_from(l).wait_recv()
        return carry

    lax.fori_loop(0, nl, finish, 0)
    for i in range(1, nd):
        part_copy(i).wait_send()
    for j in range(1, nm):
        square_copy(j, me).wait_send()
    for g in range(1, ng):
        obs_copy(2 * g, me).wait_send()
    for g in range(ng):
        obs_forward(1, cross(g), g).wait_send()
    for i in range(1, nr):
        total_copy(i, r).wait_send()
    sib_pert(c).wait_send()
    for side in (0, 1):

        @pl.when(has_side[side])
        def _():
            for g in range(ng):
                side_obs(side, cross(g), g).wait_send()
                obs_forward(2 * side, cross(g), g).wait_send()
            side_pert(side).wait_send()
            pert_forward(side, c).wait_send()
            stat_copy(side).wait_send()


def hand_on(block, out):
    pass


def solution(mesh):
    nr, nd, nm = (mesh.shape[a] for a in ("region", "depth", "member"))

    def shards(ensemble, obs_weights, obs_tiles, obs_values, obs_error, obs_noise):
        nl, mm, tt = ensemble.shape
        kk = obs_tiles.shape[0]
        ng = nm // 2
        half = tt // 2
        dma = pltpu.SemaphoreType.DMA
        vmem = pl.BlockSpec(memory_space=pltpu.VMEM)
        anywhere = pl.BlockSpec(memory_space=pl.ANY)
        analysis, inflation = pl.pallas_call(
            functools.partial(kernel, (nr, nd, nm, nl, mm, tt, kk)),
            out_shape=(
                pltpu.VMEM((nl, mm, tt), BF16),
                jax.ShapeDtypeStruct((1, 1), F32),
            ),
            in_specs=[
                pl.BlockSpec(memory_space=pltpu.SMEM),
                anywhere,
                vmem,
                vmem,
                vmem,
                anywhere,
            ],
            out_specs=(vmem, vmem),
            scratch_shapes=[
                pltpu.VMEM((nl, mm, tt), BF16),
                pltpu.VMEM((nl, nm, mm, half), BF16),
                pltpu.VMEM((mm, kk), F32),
                pltpu.VMEM((mm + 16, kk), BF16),
                pltpu.VMEM((nd, mm + 16, kk), BF16),
                pltpu.VMEM((nm, 8, kk), F32),
                pltpu.VMEM((nr, 8, 128), F32),
                pltpu.VMEM((3, 8, kk), F32),
                pltpu.VMEM((nm, mm, 3 * kk), BF16),
                pltpu.VMEM((2, mm, 3 * kk), BF16),
                pltpu.VMEM((3 * kk, nm * mm), BF16),
                pltpu.VMEM((3 * kk, half), F32),
                pltpu.VMEM((nl, nm, mm, half), BF16),
                pltpu.VMEM((nl, 8, half), F32),
                pltpu.VMEM((nl, 3 * kk, half), BF16),
                pltpu.VMEM((nl, 2, mm, half), BF16),
                dma((3,)),
                dma((nl, nm)),
                dma((nl, nm)),
                dma((nd,)),
                dma((nd,)),
                dma((nm,)),
                dma((nm,)),
                dma((nm,)),
                dma((nm,)),
                dma((nr,)),
                dma((nr,)),
                dma((2, ng)),
                dma((2, ng)),
                dma((2,)),
                dma((2,)),
                dma((1,)),
                dma((1,)),
                dma((2,)),
                dma((2,)),
                dma((2,)),
                dma((2,)),
                dma((3, ng)),
                dma((3, ng)),
                dma((nl,)),
                dma((nl,)),
                dma((nl,)),
            ],
            compiler_params=pltpu.CompilerParams(
                collective_id=0, has_side_effects=True, vmem_limit_bytes=56 * 1024 * 1024
            ),
        )(
            obs_weights,
            ensemble,
            obs_tiles.reshape(1, kk),
            obs_values.reshape(1, kk),
            obs_error.reshape(1, kk),
            obs_noise,
        )
        analysis = pl.pallas_call(
            hand_on,
            out_shape=jax.ShapeDtypeStruct((nl, mm, tt), BF16),
            in_specs=[anywhere],
            out_specs=anywhere,
            input_output_aliases={0: 0},
        )(analysis)
        return analysis, inflation.reshape(())

    return jax.shard_map(
        shards,
        mesh=mesh,
        in_specs=(
            P("depth", "member", "region"),
            P("depth"),
            P("region"),
            P("region"),
            P("region"),
            P("member", "region"),
        ),
        out_specs=(P("depth", "member", "region"), P()),
        check_vma=False,
    )
```

profile of v0, /device:TPU:0, one launch (start us, length us, event | category | flops | bytes accessed | tf_op | source)
XLA Modules:
  0.0 49.1 jit_solution(3943208805644262984)
XLA Ops:
  0.6 45.7 %shard_map.77 = (bf16[7,96,1024]{2,1,0:T(8,128)(2,1)S(1)}, f32[1,1]{1,0:T(1,128)}) custom-call(f32[7]{0:T(128)} %weights.1, bf16[7,96,1024]{2,1,0:T(8,128)(2,1)} %ensemble.1, s32[1,512]{1,0:T(1,128)} %bitcast.4, f32[1,512]{1,0:T(1,128)} %bitcast.5, f32[1,512]{1,0:T(1,128)} %bitcast.6, f32[96,512]{1,0:T(8,128)} %noise.1), custom_call_target="tpu_custom_call" | custom-call | tf_op jit(solution)/shard_map/pallas_call | solution.py:524
  46.3 1.1 %copy.12 = bf16[7,96,1024]{2,1,0:T(8,128)(2,1)} copy(bf16[7,96,1024]{2,1,0:T(8,128)(2,1)S(1)} %shard_map.78) | data formatting | bytes 2752512
  (1 shorter events, 0.0 us)
where the time goes:
time: 49.3 us; the launch traced here: 49.1 us
  Pallas kernels  45.7 us (93%)
  between operations  2.34 us (5%)
  local copies, waits for them, and re-layouts  1.08 us (2%)
    pallas_call x1, Pallas kernels, shards(): pl.pallas_call(functools.partial(kernel, (nr, nd, nm, nl, mm, tt, kk)), o...  45.7 us
    unnamed x1, local copies, waits for them, and re-layouts  1.08 us

commit v1 on v0

--- a/solution.py
+++ b/solution.py
@@ -8,7 +8,8 @@
 from jax.sharding import PartitionSpec as P
 
 RADIUS = 1024
-EARLY = 2
+LEAD = 2
+READY = 3
 F32 = jnp.float32
 BF16 = jnp.bfloat16
 MESH = pl.DeviceIdType.MESH
@@ -16,21 +17,27 @@
 
 def kernel(
     sizes,
+    weights_hbm,
+    ensemble,
+    tiles_hbm,
+    values_hbm,
+    errors_hbm,
+    noise,
+    out,
+    infl_out,
     weights,
-    ensemble,
     tiles,
     values,
     errors,
-    noise,
-    out,
-    infl_out,
     own,
     gathered,
     noise_v,
     part,
     part_in,
     squares,
-    totals,
+    tot_in,
+    tot_out,
+    pos,
     stats,
     obs,
     pert,
@@ -40,6 +47,7 @@
     means,
     gain,
     result,
+    small_sem,
     local_sem,
     send_e,
     recv_e,
@@ -55,6 +63,8 @@
     recv_z,
     send_st,
     recv_st,
+    send_pos,
+    recv_pos,
     send_ps,
     recv_ps,
     send_pz,
@@ -96,8 +106,24 @@
             device_id_type=MESH,
         )
 
+    barrier = pltpu.get_barrier_semaphore()
+    for i in range(1, nd):
+        pl.semaphore_signal(barrier, inc=1, device_id=dev(depth=(d + i) % nd), device_id_type=MESH)
+    for j in range(1, nm):
+        pl.semaphore_signal(
+            barrier, inc=1, device_id=dev(member=(me + j) % nm), device_id_type=MESH
+        )
+
     local_own = pltpu.make_async_copy(ensemble, own, local_sem.at[0])
     local_own.start()
+    smalls = [
+        pltpu.make_async_copy(a, b, small_sem.at[i])
+        for i, (a, b) in enumerate(
+            ((weights_hbm, weights), (tiles_hbm, tiles), (values_hbm, values), (errors_hbm, errors))
+        )
+    ]
+    for copy in smalls:
+        copy.start()
     local_half = pltpu.make_async_copy(
         ensemble.at[:, :, pl.ds(pl.multiple_of(c * half, 128), half)],
         gathered.at[:, me],
@@ -107,23 +133,14 @@
     local_noise = pltpu.make_async_copy(noise, noise_v, local_sem.at[2])
     local_noise.start()
 
-    group = [(i, 0) for i in range(1, nd)] + [(0, j) for j in range(1, nm)]
-    barrier = pltpu.get_barrier_semaphore()
-    signals = 0
-    for i, j in group:
-        pl.semaphore_signal(
-            barrier,
-            inc=1,
-            device_id=dev(depth=(d + i) % nd, member=(me + j) % nm),
-            device_id_type=MESH,
-        )
-        signals += 1
-    for i in range(1, nr):
-        pl.semaphore_signal(
-            barrier, inc=1, device_id=dev(region=(r + i) % nr), device_id_type=MESH
-        )
-        signals += 1
-    pl.semaphore_wait(barrier, signals)
+    pl.semaphore_wait(barrier, nd - 1 + nm - 1 + (r > 0).astype(jnp.int32))
+    for side in (0, 1):
+
+        @pl.when(has_side[side])
+        def _():
+            pl.semaphore_signal(
+                barrier, inc=1, device_id=dev(region=r + (2 * side - 1)), device_id_type=MESH
+            )
 
     def bulk(l, j):
         to = (me + j) % nm
@@ -135,11 +152,15 @@
             dev(member=to),
         )
 
-    def send_bulk(l):
+    def send_bulk(l, carry):
         for j in range(1, nm):
             bulk(l, j).start()
-
-    send_bulk(0)
+        return carry
+
+    lead = min(LEAD, nl)
+    lax.fori_loop(0, lead, send_bulk, 0)
+    for copy in smalls:
+        copy.wait()
     local_own.wait()
     total = own[0].astype(F32) * weights[0]
     for l in range(1, nl):
@@ -150,11 +171,10 @@
     low = (rest - mid.astype(F32)).astype(BF16)
     tile_ids = lax.broadcasted_iota(jnp.int32, (tt, kk), 0)
     onehot = jnp.where(tile_ids == tiles[...], 1.0, 0.0).astype(BF16)
-    picked = (
-        jnp.dot(hi, onehot, preferred_element_type=F32)
-        + jnp.dot(mid, onehot, preferred_element_type=F32)
-        + jnp.dot(low, onehot, preferred_element_type=F32)
+    terms = jnp.dot(
+        jnp.concatenate([hi, mid, low], axis=0), onehot, preferred_element_type=F32
     )
+    picked = terms[0:mm] + terms[mm : 2 * mm] + terms[2 * mm : 3 * mm]
     part_mean = jnp.sum(picked, axis=0, keepdims=True) / mm
     top = part_mean.astype(BF16).astype(F32)
     second_row = (part_mean - top).astype(BF16).astype(F32)
@@ -179,6 +199,53 @@
     for i in range(1, nd):
         part_copy(i).start()
 
+    pos[1] = jnp.broadcast_to(tiles[...].astype(F32), (8, kk))
+
+    def pos_copy(side):
+        return rdma(
+            pos.at[1],
+            pos.at[2 - 2 * side],
+            send_pos.at[side],
+            recv_pos.at[1 - side],
+            dev(region=r + (2 * side - 1)),
+        )
+
+    def pos_from(side):
+        return rdma(
+            pos.at[1],
+            pos.at[2 * side],
+            send_pos.at[side],
+            recv_pos.at[side],
+            dev(region=r + (2 * side - 1)),
+        )
+
+    lane = (lax.broadcasted_iota(jnp.int32, (kk, half), 1) + c * half).astype(F32)
+
+    def make_taper(w):
+        position = pos[w].T[:, 0:1] + float((w - 1) * tt)
+        close = jnp.maximum(0.0, 1.0 - jnp.abs(lane - position) * (1.0 / RADIUS))
+        taper[w * kk : (w + 1) * kk] = close * close
+
+    make_taper(1)
+
+    @pl.when(has_side[1])
+    def _():
+        pl.semaphore_wait(barrier, 1)
+
+    for side in (0, 1):
+
+        @pl.when(has_side[side])
+        def _():
+            pos_copy(side).start()
+
+        @pl.when(jnp.logical_not(has_side[side]))
+        def _():
+            window = 0 if side == 0 else 2 * kk
+            obs[:, :, window : window + kk] = jnp.zeros((nm, mm, kk), BF16)
+            pert[:, :, window : window + kk] = jnp.zeros((2, mm, kk), BF16)
+            stats[2 * side] = jnp.zeros((8, kk), F32)
+            pos[2 * side] = jnp.zeros((8, kk), F32)
+
     predicted = whole(part[...])
     for i in range(1, nd):
         part_from(i).wait_recv()
@@ -186,8 +253,8 @@
     own_sum = jnp.sum(predicted, axis=0, keepdims=True)
     spread_in = predicted - own_sum / mm
     own_square = jnp.sum(spread_in * spread_in, axis=0, keepdims=True)
-    krow = lax.broadcasted_iota(jnp.int32, (8, kk), 0)
-    squares[me] = jnp.where(krow == 0, own_sum, own_square)
+    qrow = lax.broadcasted_iota(jnp.int32, (2, kk), 0)
+    squares[me] = jnp.where(qrow == 0, own_sum, own_square)
     obs[me, :, kk : 2 * kk] = spread_in.astype(BF16)
 
     def square_copy(j, slot):
@@ -228,24 +295,15 @@
     for g in range(1, ng):
         obs_copy(2 * g, me).start()
     obs_forward(1, me, 0).start()
+    lax.fori_loop(lead, nl, send_bulk, 0)
     for side in (0, 1):
 
         @pl.when(has_side[side])
         def _():
             side_obs(side, me, 0).start()
-
-        @pl.when(jnp.logical_not(has_side[side]))
-        def _():
-            window = 0 if side == 0 else 2 * kk
-            obs[:, :, window : window + kk] = jnp.zeros((nm, mm, kk), BF16)
-            pert[:, :, window : window + kk] = jnp.zeros((2, mm, kk), BF16)
-            stats[2 * side] = jnp.zeros((8, kk), F32)
-
-    def send_rest(l, carry):
-        send_bulk(l)
-        return carry
-
-    lax.fori_loop(1, nl, send_rest, 0)
+            pos_from(side).wait_recv()
+
+        make_taper(2 * side)
 
     for j in range(1, nm):
         square_copy(j, (me + j) % nm).wait_recv()
@@ -260,48 +318,15 @@
     innovation = values[...] - obs_mean
     first = jnp.sum(innovation * innovation, axis=1, keepdims=True)
     second = jnp.sum(spread + error, axis=1, keepdims=True)
-    rows = lax.broadcasted_iota(jnp.int32, (8, 128), 0)
-    totals[r] = jnp.where(rows == 0, first, second)
-
-    def total_copy(i, slot):
-        return rdma(
-            totals.at[slot],
-            totals.at[slot],
-            send_g.at[i],
-            recv_g.at[slot],
-            dev(region=(r + i) % nr),
-        )
-
-    for i in range(1, nr):
-        total_copy(i, r).start()
-
-    for g in range(1, ng):
-        obs_copy(2 * g, cross(g)).wait_recv()
-        for side in (0, 1):
-
-            @pl.when(has_side[side])
-            def _():
-                side_obs(side, cross(g), g).start()
-
-        obs_forward(1, cross(g), g).start()
-
-    for i in range(1, nr):
-        total_copy(i, (r + i) % nr).wait_recv()
-    grand = totals[0]
-    for i in range(1, nr):
-        grand = grand + totals[i]
-    inflation = grand[0:1, 0:1] / grand[1:2, 0:1]
-    root = jnp.sqrt(inflation)
-    infl_out[...] = inflation
-    factor = inflation / (inflation * spread + error)
-    facts = jnp.where(krow == 0, tiles[...].astype(F32), factor / (members - 1))
+    rp = tot_in.shape[1]
+    trow = lax.broadcasted_iota(jnp.int32, (rp, 128), 0)
+    tlane = lax.broadcasted_iota(jnp.int32, (rp, 128), 1)
+    own_total = jnp.where(tlane == 0, first, second)
+    krow = lax.broadcasted_iota(jnp.int32, (8, kk), 0)
+    shifts_of = jnp.zeros((8, kk), F32)
     for g in range(nm):
-        facts = jnp.where(krow == 2 + g, moments[g][0:1] / mm - obs_mean, facts)
-    stats[1] = facts
-    local_noise.wait()
-    pert[c, :, kk : 2 * kk] = (
-        innovation + jnp.sqrt(error) * noise_v[...] - root * deviation
-    ).astype(BF16)
+        shifts_of = jnp.where(krow == g, moments[g][0:1] / mm - obs_mean, shifts_of)
+    stats[1] = shifts_of
 
     def stat_copy(side):
         return rdma(
@@ -312,61 +337,79 @@
             dev(region=r + (2 * side - 1)),
         )
 
-    def sib_pert(slot):
-        block = pert.at[slot, :, pl.ds(kk, kk)]
-        return rdma(block, block, send_ps.at[0], recv_ps.at[0], dev(member=sib))
-
-    def side_pert(side):
-        window = 2 * kk if side == 0 else 0
-        return rdma(
-            pert.at[c, :, pl.ds(kk, kk)],
-            pert.at[c, :, pl.ds(window, kk)],
-            send_pz.at[side],
-            recv_pz.at[1 - side],
-            dev(region=r + (2 * side - 1)),
-        )
-
-    def pert_forward(side, slot):
-        block = pert.at[slot, :, pl.ds(2 * kk * side, kk)]
-        return rdma(block, block, send_pf.at[side], recv_pf.at[side], dev(member=sib))
-
-    sib_pert(c).start()
+    def total_copy(way):
+        return rdma(
+            tot_out.at[way],
+            tot_in.at[way],
+            send_g.at[way],
+            recv_g.at[way],
+            dev(region=r + (1 - 2 * way)),
+        )
+
+    def total_from(way):
+        return rdma(
+            tot_out.at[way],
+            tot_in.at[way],
+            send_g.at[way],
+            recv_g.at[way],
+            dev(region=r - (1 - 2 * way)),
+        )
+
+    def relay(way):
+        @pl.when(has_side[way])
+        def _():
+            total_from(way).wait_recv()
+
+        behind = trow < r if way == 0 else trow > r
+        tot_out[way] = jnp.where(
+            behind, tot_in[way], jnp.where(trow == r, own_total, 0.0)
+        )
+
+        @pl.when(has_side[1 - way])
+        def _():
+            total_copy(way).start()
+
+    low_end = r == 0
+    high_end = r == nr - 1
+
+    @pl.when(low_end)
+    def _():
+        relay(0)
+
+    @pl.when(high_end)
+    def _():
+        relay(1)
+
     for side in (0, 1):
 
         @pl.when(has_side[side])
         def _():
             stat_copy(side).start()
-            side_pert(side).start()
-
-    lane = (lax.broadcasted_iota(jnp.int32, (kk, half), 1) + c * half).astype(F32)
-
-    def make_taper(w):
-        columns = stats[w].T
-        position = columns[:, 0:1] + float((w - 1) * tt)
-        close = jnp.maximum(0.0, 1.0 - jnp.abs(lane - position) * (1.0 / RADIUS))
-        taper[w * kk : (w + 1) * kk] = close * close * columns[:, 1:2]
+
+    for g in range(1, ng):
+        obs_copy(2 * g, cross(g)).wait_recv()
+        for side in (0, 1):
+
+            @pl.when(has_side[side])
+            def _():
+                side_obs(side, cross(g), g).start()
+
+        obs_forward(1, cross(g), g).start()
 
     def transpose_all(w):
         shifts = stats[w].T
         for g in range(nm):
-            block = obs[g, :, w * kk : (w + 1) * kk].astype(F32).T + shifts[:, 2 + g : 3 + g]
+            block = obs[g, :, w * kk : (w + 1) * kk].astype(F32).T + shifts[:, g : g + 1]
             obs_t[w * kk : (w + 1) * kk, g * mm : (g + 1) * mm] = block.astype(BF16)
 
-    step = kk // 2
-
-    def gain_blocks(l, lo, hi):
+    def gain_rows(l, windows):
         right = anom[l].reshape(members, half)
-
-        def one_block(b, inner):
-            at = (b + 2 * (b // 2)) if lo == 0 else b
-            rows_of = pl.ds(pl.multiple_of(at * step, step), step)
+        for w in windows:
+            rows_of = slice(w * kk, (w + 1) * kk)
             cov = jnp.dot(obs_t[rows_of], right, preferred_element_type=F32)
             gain[l, rows_of] = (cov * taper[rows_of]).astype(BF16)
-            return inner
-
-        lax.fori_loop(lo, hi, one_block, 0)
-
-    def own_window(l, carry):
+
+    def own_window(l, windows):
         for j in range(1, nm):
             slot = (me + j) % nm
             rdma(
@@ -380,16 +423,71 @@
         mean = jnp.sum(jnp.sum(raw, axis=0), axis=0, keepdims=True) / members
         means[l] = jnp.broadcast_to(mean, (8, half))
         anom[l] = (raw - mean[None]).astype(BF16)
-        gain_blocks(l, 2, 4)
-        return carry
-
-    make_taper(1)
+        gain_rows(l, windows)
+
     for g in range(ng):
         obs_forward(1, cross_sib(g), g).wait_recv()
     transpose_all(1)
+    mid_low = jnp.logical_and(r > 0, 2 * r < nr)
+    mid_high = jnp.logical_and(r < nr - 1, 2 * r >= nr)
+
+    @pl.when(mid_low)
+    def _():
+        relay(0)
+
+    @pl.when(mid_high)
+    def _():
+        relay(1)
+
     local_half.wait()
-    early = min(EARLY, nl)
-    own_window(0, 0)
+    own_window(0, (1,))
+
+    @pl.when(2 * r < nr)
+    def _():
+        relay(1)
+
+    @pl.when(2 * r >= nr)
+    def _():
+        relay(0)
+
+    everyone = jnp.where(trow < r, tot_in[0], jnp.where(trow > r, tot_in[1], own_total))
+    grand = everyone[0:1]
+    for i in range(1, nr):
+        grand = grand + everyone[i : i + 1]
+    inflation = grand[0:1, 0:1] / grand[0:1, 1:2]
+    root = jnp.sqrt(inflation)
+    infl_out[...] = inflation
+    factor = inflation / (inflation * spread + error)
+    local_noise.wait()
+    pert[c, :, kk : 2 * kk] = (
+        (innovation + jnp.sqrt(error) * noise_v[...] - root * deviation)
+        * (factor / (members - 1))
+    ).astype(BF16)
+
+    def sib_pert(slot):
+        block = pert.at[slot, :, pl.ds(kk, kk)]
+        return rdma(block, block, send_ps.at[0], recv_ps.at[0], dev(member=sib))
+
+    def side_pert(side):
+        window = 2 * kk if side == 0 else 0
+        return rdma(
+            pert.at[c, :, pl.ds(kk, kk)],
+            pert.at[c, :, pl.ds(window, kk)],
+            send_pz.at[side],
+            recv_pz.at[1 - side],
+            dev(region=r + (2 * side - 1)),
+        )
+
+    def pert_forward(side, slot):
+        block = pert.at[slot, :, pl.ds(2 * kk * side, kk)]
+        return rdma(block, block, send_pf.at[side], recv_pf.at[side], dev(member=sib))
+
+    sib_pert(c).start()
+    for side in (0, 1):
+
+        @pl.when(has_side[side])
+        def _():
+            side_pert(side).start()
 
     for g in range(ng):
         for side in (0, 1):
@@ -399,6 +497,7 @@
                 side_obs(1 - side, cross(g), g).wait_recv()
                 obs_forward(2 * side, cross(g), g).start()
 
+    own_window(1, (1,))
     for side in (0, 1):
 
         @pl.when(has_side[side])
@@ -410,13 +509,6 @@
                 recv_st.at[side],
                 dev(region=r + (2 * side - 1)),
             ).wait_recv()
-
-        make_taper(2 * side)
-
-    for side in (0, 1):
-
-        @pl.when(has_side[side])
-        def _():
             for g in range(ng):
                 obs_forward(2 * side, cross_sib(g), g).wait_recv()
 
@@ -438,31 +530,7 @@
             result.at[l, 1 - c], out_half(l, 1 - c), send_out.at[l], recv_out.at[l], dev(member=sib)
         )
 
-    def one_variable(l, carry):
-        @pl.when(l >= early)
-        def _():
-            own_window(l, 0)
-
-        gain_blocks(l, 0, 4)
-
-        @pl.when(l == 0)
-        def _():
-            for side in (0, 1):
-
-                @pl.when(has_side[side])
-                def _():
-                    side_pert(1 - side).wait_recv()
-                    pert_forward(side, c).start()
-
-            for ahead in range(1, early):
-                own_window(ahead, 0)
-            sib_pert(1 - c).wait_recv()
-            for side in (0, 1):
-
-                @pl.when(has_side[side])
-                def _():
-                    pert_forward(side, 1 - c).wait_recv()
-
+    def finish_variable(l):
         increment = jnp.dot(
             pert[...].reshape(2 * mm, 3 * kk), gain[l], preferred_element_type=F32
         )
@@ -470,9 +538,45 @@
         result[l] = (base + increment.reshape(2, mm, half)).astype(BF16)
         out_local(l).start()
         out_remote(l).start()
+
+    def side_gain(l, carry):
+        gain_rows(l, (0, 2))
         return carry
 
-    lax.fori_loop(0, nl, one_variable, 0)
+    lax.fori_loop(0, 2, side_gain, 0)
+    for side in (0, 1):
+
+        @pl.when(has_side[side])
+        def _():
+            side_pert(1 - side).wait_recv()
+            pert_forward(side, c).start()
+
+    ready = min(READY, nl)
+
+    def ahead(l, carry):
+        own_window(l, (0, 1, 2))
+        return carry
+
+    lax.fori_loop(2, ready, ahead, 0)
+    sib_pert(1 - c).wait_recv()
+    for side in (0, 1):
+
+        @pl.when(has_side[side])
+        def _():
+            pert_forward(side, 1 - c).wait_recv()
+
+    def late_variable(l, carry):
+        finish_variable(l)
+        return carry
+
+    lax.fori_loop(0, ready, late_variable, 0)
+
+    def one_variable(l, carry):
+        own_window(l, (0, 1, 2))
+        finish_variable(l)
+        return carry
+
+    lax.fori_loop(ready, nl, one_variable, 0)
 
     def finish(l, carry):
         for j in range(1, nm):
@@ -491,9 +595,13 @@
         obs_copy(2 * g, me).wait_send()
     for g in range(ng):
         obs_forward(1, cross(g), g).wait_send()
-    for i in range(1, nr):
-        total_copy(i, r).wait_send()
     sib_pert(c).wait_send()
+    for way in (0, 1):
+
+        @pl.when(has_side[1 - way])
+        def _():
+            total_copy(way).wait_send()
+
     for side in (0, 1):
 
         @pl.when(has_side[side])
@@ -504,6 +612,7 @@
             side_pert(side).wait_send()
             pert_forward(side, c).wait_send()
             stat_copy(side).wait_send()
+            pos_copy(side).wait_send()
 
 
 def hand_on(block, out):
@@ -518,6 +627,7 @@
         kk = obs_tiles.shape[0]
         ng = nm // 2
         half = tt // 2
+        rp = -(-nr // 8) * 8
         dma = pltpu.SemaphoreType.DMA
         vmem = pl.BlockSpec(memory_space=pltpu.VMEM)
         anywhere = pl.BlockSpec(memory_space=pl.ANY)
@@ -527,23 +637,22 @@
                 pltpu.VMEM((nl, mm, tt), BF16),
                 jax.ShapeDtypeStruct((1, 1), F32),
             ),
-            in_specs=[
-                pl.BlockSpec(memory_space=pltpu.SMEM),
-                anywhere,
-                vmem,
-                vmem,
-                vmem,
-                anywhere,
-            ],
+            in_specs=[anywhere] * 6,
             out_specs=(vmem, vmem),
             scratch_shapes=[
+                pltpu.SMEM((nl,), F32),
+                pltpu.VMEM((1, kk), jnp.int32),
+                pltpu.VMEM((1, kk), F32),
+                pltpu.VMEM((1, kk), F32),
                 pltpu.VMEM((nl, mm, tt), BF16),
                 pltpu.VMEM((nl, nm, mm, half), BF16),
                 pltpu.VMEM((mm, kk), F32),
                 pltpu.VMEM((mm + 16, kk), BF16),
                 pltpu.VMEM((nd, mm + 16, kk), BF16),
-                pltpu.VMEM((nm, 8, kk), F32),
-                pltpu.VMEM((nr, 8, 128), F32),
+                pltpu.VMEM((nm, 2, kk), F32),
+                pltpu.VMEM((2, rp, 128), F32),
+                pltpu.VMEM((2, rp, 128), F32),
+                pltpu.VMEM((3, 8, kk), F32),
                 pltpu.VMEM((3, 8, kk), F32),
                 pltpu.VMEM((nm, mm, 3 * kk), BF16),
                 pltpu.VMEM((2, mm, 3 * kk), BF16),
@@ -553,6 +662,7 @@
                 pltpu.VMEM((nl, 8, half), F32),
                 pltpu.VMEM((nl, 3 * kk, half), BF16),
                 pltpu.VMEM((nl, 2, mm, half), BF16),
+                dma((4,)),
                 dma((3,)),
                 dma((nl, nm)),
                 dma((nl, nm)),
@@ -562,10 +672,12 @@
                 dma((nm,)),
                 dma((nm,)),
                 dma((nm,)),
-                dma((nr,)),
-                dma((nr,)),
+                dma((2,)),
+                dma((2,)),
                 dma((2, ng)),
                 dma((2, ng)),
+                dma((2,)),
+                dma((2,)),
                 dma((2,)),
                 dma((2,)),
                 dma((1,)),

time: 49.3 us -> 44.5 us (0.903)
  Pallas kernels: 45.7 us -> 40.9 us
    pallas_call x1, Pallas kernels: 45.7 us -> 40.9 us  [shards(): pl.pallas_call(functools.partial(kernel, (nr, nd, nm, nl, mm, tt, kk)), o...]
where the time goes in v1:
time: 44.5 us; the launch traced here: 44.3 us
  Pallas kernels  40.9 us (92%)
  between operations  2.34 us (5%)
  local copies, waits for them, and re-layouts  1.08 us (2%)
    pallas_call x1, Pallas kernels, shards(): pl.pallas_call(functools.partial(kernel, (nr, nd, nm, nl, mm, tt, kk)), o...  40.9 us
    unnamed x1, local copies, waits for them, and re-layouts  1.08 us

profile of v1, /device:TPU:0, one launch (start us, length us, event | category | flops | bytes accessed | tf_op | source)
XLA Modules:
  0.0 44.3 jit_solution(16493024479962711293)
XLA Ops:
  0.6 40.9 %shard_map.77 = (bf16[7,96,1024]{2,1,0:T(8,128)(2,1)S(1)}, f32[1,1]{1,0:T(1,128)}) custom-call(f32[7]{0:T(128)} %weights_hbm.1, bf16[7,96,1024]{2,1,0:T(8,128)(2,1)} %ensemble.1, s32[1,512]{1,0:T(1,128)} %bitcast.4, f32[1,512]{1,0:T(1,128)} %bitcast.5, f32[1,512]{1,0:T(1,128)} %bitcast.6, f32[96,512]{1,0:T(8,128)} %noise.1), custom_call_target="tpu_custom_call" | custom-call | tf_op jit(solution)/shard_map/pallas_call | solution.py:634
  41.6 1.1 %copy.12 = bf16[7,96,1024]{2,1,0:T(8,128)(2,1)} copy(bf16[7,96,1024]{2,1,0:T(8,128)(2,1)S(1)} %shard_map.78) | data formatting | bytes 2752512
  (1 shorter events, 0.0 us)

commit v2 on v1

--- a/solution.py
+++ b/solution.py
@@ -8,8 +8,9 @@
 from jax.sharding import PartitionSpec as P
 
 RADIUS = 1024
-LEAD = 2
-READY = 3
+LEAD = 3
+READY = 5
+PIECES = 2
 F32 = jnp.float32
 BF16 = jnp.bfloat16
 MESH = pl.DeviceIdType.MESH
@@ -47,6 +48,8 @@
     means,
     gain,
     result,
+    scale,
+    answer,
     small_sem,
     local_sem,
     send_e,
@@ -59,6 +62,8 @@
     recv_o,
     send_g,
     recv_g,
+    send_y,
+    recv_y,
     send_z,
     recv_z,
     send_st,
@@ -107,12 +112,19 @@
         )
 
     barrier = pltpu.get_barrier_semaphore()
-    for i in range(1, nd):
-        pl.semaphore_signal(barrier, inc=1, device_id=dev(depth=(d + i) % nd), device_id_type=MESH)
     for j in range(1, nm):
         pl.semaphore_signal(
             barrier, inc=1, device_id=dev(member=(me + j) % nm), device_id_type=MESH
         )
+    for i in range(1, nd):
+
+        @pl.when(d + i < nd)
+        def _():
+            pl.semaphore_signal(barrier, inc=1, device_id=dev(depth=d + i), device_id_type=MESH)
+
+    @pl.when(has_side[1])
+    def _():
+        pl.semaphore_signal(barrier, inc=1, device_id=dev(region=r + 1), device_id_type=MESH)
 
     local_own = pltpu.make_async_copy(ensemble, own, local_sem.at[0])
     local_own.start()
@@ -133,32 +145,47 @@
     local_noise = pltpu.make_async_copy(noise, noise_v, local_sem.at[2])
     local_noise.start()
 
-    pl.semaphore_wait(barrier, nd - 1 + nm - 1 + (r > 0).astype(jnp.int32))
-    for side in (0, 1):
-
-        @pl.when(has_side[side])
+    pl.semaphore_wait(barrier, nm - 1 + d + (r > 0).astype(jnp.int32))
+
+    piece = half // PIECES
+    units = nl * PIECES
+
+    def bulk(u, j):
+        to = (me + j) % nm
+        l, at = u // PIECES, (u % PIECES) * piece
+        return rdma(
+            ensemble.at[l, :, pl.ds(pl.multiple_of((to % 2) * half + at, 128), piece)],
+            gathered.at[l, me, :, pl.ds(pl.multiple_of(at, 128), piece)],
+            send_e.at[u, j],
+            recv_e.at[u, me],
+            dev(member=to),
+        )
+
+    def bulk_from(u, j):
+        slot = (me + j) % nm
+        l, at = u // PIECES, (u % PIECES) * piece
+        block = gathered.at[l, slot, :, pl.ds(pl.multiple_of(at, 128), piece)]
+        return rdma(block, block, send_e.at[u, j], recv_e.at[u, slot], dev(member=slot))
+
+    def send_bulk(u, carry):
+        for j in range(1, nm):
+            bulk(u, j).start()
+        return carry
+
+    lead = min(LEAD, units)
+    lax.fori_loop(0, lead, send_bulk, 0)
+    for i in range(1, nd):
+
+        @pl.when(d >= i)
         def _():
             pl.semaphore_signal(
-                barrier, inc=1, device_id=dev(region=r + (2 * side - 1)), device_id_type=MESH
+                answer.at[0], inc=1, device_id=dev(depth=d - i), device_id_type=MESH
             )
 
-    def bulk(l, j):
-        to = (me + j) % nm
-        return rdma(
-            ensemble.at[l, :, pl.ds(pl.multiple_of((to % 2) * half, 128), half)],
-            gathered.at[l, me],
-            send_e.at[l, j],
-            recv_e.at[l, me],
-            dev(member=to),
-        )
-
-    def send_bulk(l, carry):
-        for j in range(1, nm):
-            bulk(l, j).start()
-        return carry
-
-    lead = min(LEAD, nl)
-    lax.fori_loop(0, lead, send_bulk, 0)
+    @pl.when(has_side[0])
+    def _():
+        pl.semaphore_signal(answer.at[1], inc=1, device_id=dev(region=r - 1), device_id_type=MESH)
+
     for copy in smalls:
         copy.wait()
     local_own.wait()
@@ -196,6 +223,10 @@
         frm = (d + i) % nd
         return rdma(part, part_in.at[frm], send_p.at[i], recv_p.at[frm], dev(depth=frm))
 
+    @pl.when(d < nd - 1)
+    def _():
+        pl.semaphore_wait(answer.at[0], nd - 1 - d)
+
     for i in range(1, nd):
         part_copy(i).start()
 
@@ -230,7 +261,7 @@
 
     @pl.when(has_side[1])
     def _():
-        pl.semaphore_wait(barrier, 1)
+        pl.semaphore_wait(answer.at[1], 1)
 
     for side in (0, 1):
 
@@ -266,23 +297,43 @@
             dev(member=(me + j) % nm),
         )
 
+    hk = kk // nd
+
+    def obs_at(slot, w, h, width):
+        return obs.at[slot, :, pl.ds(pl.multiple_of(w * kk + h * hk, 128), width)]
+
     def obs_copy(j, slot):
-        block = obs.at[slot, :, pl.ds(kk, kk)]
+        block = obs_at(slot, 1, d, hk)
         return rdma(block, block, send_o.at[j], recv_o.at[slot], dev(member=(me + j) % nm))
 
-    def side_obs(side, slot, pair):
-        window = 2 * kk if side == 0 else 0
-        return rdma(
-            obs.at[slot, :, pl.ds(kk, kk)],
-            obs.at[slot, :, pl.ds(window, kk)],
-            send_z.at[side, pair],
-            recv_z.at[1 - side, pair],
+    def obs_swap(g, i, h):
+        block = obs_at(cross(g), 1, h, hk)
+        return rdma(block, block, send_y.at[g, i], recv_y.at[g, h], dev(depth=(d + i) % nd))
+
+    def side_obs(side, slot, pair, h, width):
+        return rdma(
+            obs_at(slot, 1, h, width),
+            obs_at(slot, 2 if side == 0 else 0, h, width),
+            send_z.at[side, pair, h],
+            recv_z.at[1 - side, pair, h],
             dev(region=r + (2 * side - 1)),
         )
 
-    def obs_forward(w, slot, pair):
-        block = obs.at[slot, :, pl.ds(w * kk, kk)]
-        return rdma(block, block, send_f.at[w, pair], recv_f.at[w, pair], dev(member=sib))
+    def side_from(side, slot, pair, h, width):
+        block = obs_at(slot, 2 * side, h, width)
+        return rdma(
+            block,
+            block,
+            send_z.at[side, pair, h],
+            recv_z.at[side, pair, h],
+            dev(region=r + (2 * side - 1)),
+        )
+
+    def obs_forward(w, slot, pair, h, width):
+        block = obs_at(slot, w, h, width)
+        return rdma(
+            block, block, send_f.at[w, pair, h], recv_f.at[w, pair, h], dev(member=sib)
+        )
 
     def cross(g):
         return 2 * ((q + g) % ng) + c
@@ -294,13 +345,13 @@
         square_copy(j, me).start()
     for g in range(1, ng):
         obs_copy(2 * g, me).start()
-    obs_forward(1, me, 0).start()
-    lax.fori_loop(lead, nl, send_bulk, 0)
+    obs_forward(1, me, 0, 0, kk).start()
+    lax.fori_loop(lead, units, send_bulk, 0)
     for side in (0, 1):
 
         @pl.when(has_side[side])
         def _():
-            side_obs(side, me, 0).start()
+            side_obs(side, me, 0, 0, kk).start()
             pos_from(side).wait_recv()
 
         make_taper(2 * side)
@@ -386,83 +437,52 @@
         def _():
             stat_copy(side).start()
 
+    def hand_part(g, h):
+        for side in (0, 1):
+
+            @pl.when(has_side[side])
+            def _():
+                side_obs(side, cross(g), g, h, hk).start()
+
+        obs_forward(1, cross(g), g, h, hk).start()
+
     for g in range(1, ng):
         obs_copy(2 * g, cross(g)).wait_recv()
-        for side in (0, 1):
-
-            @pl.when(has_side[side])
-            def _():
-                side_obs(side, cross(g), g).start()
-
-        obs_forward(1, cross(g), g).start()
-
-    def transpose_all(w):
-        shifts = stats[w].T
+        for i in range(1, nd):
+            obs_swap(g, i, d).start()
+        hand_part(g, d)
+
+    def transpose_part(w, h, width):
+        at = pl.multiple_of(h * hk, 128)
+        rows_of = pl.ds(pl.multiple_of(w * kk + at, 128), width)
+        shifts = stats[w, :, pl.ds(at, width)].T
         for g in range(nm):
-            block = obs[g, :, w * kk : (w + 1) * kk].astype(F32).T + shifts[:, g : g + 1]
-            obs_t[w * kk : (w + 1) * kk, g * mm : (g + 1) * mm] = block.astype(BF16)
-
-    def gain_rows(l, windows):
-        right = anom[l].reshape(members, half)
+            block = obs[g, :, rows_of].astype(F32).T + shifts[:, g : g + 1]
+            obs_t[rows_of, g * mm : (g + 1) * mm] = block.astype(BF16)
+
+    everything = (0, half)
+
+    def gain_rows(l, windows, columns=everything):
+        cols = slice(*columns)
+        right = anom[l, :, :, cols].reshape(members, columns[1] - columns[0])
         for w in windows:
             rows_of = slice(w * kk, (w + 1) * kk)
             cov = jnp.dot(obs_t[rows_of], right, preferred_element_type=F32)
-            gain[l, rows_of] = (cov * taper[rows_of]).astype(BF16)
-
-    def own_window(l, windows):
-        for j in range(1, nm):
-            slot = (me + j) % nm
-            rdma(
-                gathered.at[l, slot],
-                gathered.at[l, slot],
-                send_e.at[l, j],
-                recv_e.at[l, slot],
-                dev(member=slot),
-            ).wait_recv()
-        raw = gathered[l].astype(F32)
+            gain[l, rows_of, cols] = (cov * taper[rows_of, cols]).astype(BF16)
+
+    def center(l, columns=everything):
+        cols = slice(*columns)
+        for u in range(columns[0] // piece, columns[1] // piece):
+            for j in range(1, nm):
+                bulk_from(l * PIECES + u, j).wait_recv()
+        raw = gathered[l, :, :, cols].astype(F32)
         mean = jnp.sum(jnp.sum(raw, axis=0), axis=0, keepdims=True) / members
-        means[l] = jnp.broadcast_to(mean, (8, half))
-        anom[l] = (raw - mean[None]).astype(BF16)
-        gain_rows(l, windows)
-
-    for g in range(ng):
-        obs_forward(1, cross_sib(g), g).wait_recv()
-    transpose_all(1)
-    mid_low = jnp.logical_and(r > 0, 2 * r < nr)
-    mid_high = jnp.logical_and(r < nr - 1, 2 * r >= nr)
-
-    @pl.when(mid_low)
-    def _():
-        relay(0)
-
-    @pl.when(mid_high)
-    def _():
-        relay(1)
-
-    local_half.wait()
-    own_window(0, (1,))
-
-    @pl.when(2 * r < nr)
-    def _():
-        relay(1)
-
-    @pl.when(2 * r >= nr)
-    def _():
-        relay(0)
-
-    everyone = jnp.where(trow < r, tot_in[0], jnp.where(trow > r, tot_in[1], own_total))
-    grand = everyone[0:1]
-    for i in range(1, nr):
-        grand = grand + everyone[i : i + 1]
-    inflation = grand[0:1, 0:1] / grand[0:1, 1:2]
-    root = jnp.sqrt(inflation)
-    infl_out[...] = inflation
-    factor = inflation / (inflation * spread + error)
-    local_noise.wait()
-    pert[c, :, kk : 2 * kk] = (
-        (innovation + jnp.sqrt(error) * noise_v[...] - root * deviation)
-        * (factor / (members - 1))
-    ).astype(BF16)
+        means[l, :, cols] = jnp.broadcast_to(mean, (8, columns[1] - columns[0]))
+        anom[l, :, :, cols] = (raw - mean[None]).astype(BF16)
+
+    def own_window(l, windows, columns=everything):
+        center(l, columns)
+        gain_rows(l, windows, columns)
 
     def sib_pert(slot):
         block = pert.at[slot, :, pl.ds(kk, kk)]
@@ -482,22 +502,82 @@
         block = pert.at[slot, :, pl.ds(2 * kk * side, kk)]
         return rdma(block, block, send_pf.at[side], recv_pf.at[side], dev(member=sib))
 
-    sib_pert(c).start()
-    for side in (0, 1):
-
-        @pl.when(has_side[side])
-        def _():
-            side_pert(side).start()
-
-    for g in range(ng):
+    def make_pert():
+        everyone = jnp.where(trow < r, tot_in[0], jnp.where(trow > r, tot_in[1], own_total))
+        grand = everyone[0:1]
+        for i in range(1, nr):
+            grand = grand + everyone[i : i + 1]
+        inflation = grand[0:1, 0:1] / grand[0:1, 1:2]
+        root = jnp.sqrt(inflation)
+        infl_out[...] = inflation
+        scale[...] = jnp.broadcast_to(root, (1, 128))
+        factor = inflation / (inflation * spread + error)
+        local_noise.wait()
+        pert[c, :, kk : 2 * kk] = (
+            (innovation + jnp.sqrt(error) * noise_v[...] - root * deviation)
+            * (factor / (members - 1))
+        ).astype(BF16)
+
+        sib_pert(c).start()
         for side in (0, 1):
 
             @pl.when(has_side[side])
             def _():
-                side_obs(1 - side, cross(g), g).wait_recv()
-                obs_forward(2 * side, cross(g), g).start()
-
-    own_window(1, (1,))
+                side_pert(side).start()
+
+    mid_low = jnp.logical_and(r > 0, 2 * r < nr)
+    mid_high = jnp.logical_and(r < nr - 1, 2 * r >= nr)
+
+    @pl.when(mid_low)
+    def _():
+        relay(0)
+
+    @pl.when(mid_high)
+    def _():
+        relay(1)
+
+    obs_forward(1, sib, 0, 0, kk).wait_recv()
+    for g in range(1, ng):
+        obs_forward(1, cross_sib(g), g, d, hk).wait_recv()
+    transpose_part(1, d, hk)
+    local_half.wait()
+    center(0)
+    for i in range(1, nd):
+        h = (d + i) % nd
+        for g in range(1, ng):
+            obs_swap(g, i, h).wait_recv()
+            hand_part(g, h)
+    center(1)
+    for i in range(1, nd):
+        h = (d + i) % nd
+        for g in range(1, ng):
+            obs_forward(1, cross_sib(g), g, h, hk).wait_recv()
+        transpose_part(1, h, hk)
+    gain_rows(0, (1,))
+
+    for side in (0, 1):
+
+        @pl.when(has_side[side])
+        def _():
+            side_from(side, me, 0, 0, kk).wait_recv()
+            obs_forward(2 * side, me, 0, 0, kk).start()
+            for g in range(1, ng):
+                for h in range(nd):
+                    side_from(side, cross(g), g, h, hk).wait_recv()
+                obs_forward(2 * side, cross(g), g, 0, kk).start()
+
+    gain_rows(1, (1,))
+
+    @pl.when(mid_low)
+    def _():
+        relay(1)
+        make_pert()
+
+    @pl.when(mid_high)
+    def _():
+        relay(0)
+        make_pert()
+
     for side in (0, 1):
 
         @pl.when(has_side[side])
@@ -510,40 +590,68 @@
                 dev(region=r + (2 * side - 1)),
             ).wait_recv()
             for g in range(ng):
-                obs_forward(2 * side, cross_sib(g), g).wait_recv()
-
-        transpose_all(2 * side)
-
-    def out_half(l, which):
-        return out.at[l, :, pl.ds(pl.multiple_of(which * half, 128), half)]
-
-    def out_local(l):
-        return pltpu.make_async_copy(result.at[l, c], out_half(l, c), own_out.at[l])
-
-    def out_remote(l):
-        return rdma(
-            result.at[l, 1 - c], out_half(l, c), send_out.at[l], recv_out.at[l], dev(member=sib)
-        )
-
-    def out_from(l):
-        return rdma(
-            result.at[l, 1 - c], out_half(l, 1 - c), send_out.at[l], recv_out.at[l], dev(member=sib)
-        )
-
-    def finish_variable(l):
+                obs_forward(2 * side, cross_sib(g), g, 0, kk).wait_recv()
+
+        transpose_part(2 * side, 0, kk)
+
+    def out_block(l, which, p):
+        at = which * half + p * piece
+        return out.at[l, :, pl.ds(pl.multiple_of(at, 128), piece)]
+
+    def out_piece(l, which, p):
+        return result.at[l, which, :, p * piece : (p + 1) * piece]
+
+    def out_local(l, p):
+        return pltpu.make_async_copy(out_piece(l, c, p), out_block(l, c, p), own_out.at[l, p])
+
+    def out_remote(l, p):
+        return rdma(
+            out_piece(l, 1 - c, p),
+            out_block(l, c, p),
+            send_out.at[l, p],
+            recv_out.at[l, p],
+            dev(member=sib),
+        )
+
+    def out_from(l, p):
+        return rdma(
+            out_piece(l, 1 - c, p),
+            out_block(l, 1 - c, p),
+            send_out.at[l, p],
+            recv_out.at[l, p],
+            dev(member=sib),
+        )
+
+    def finish_variable(l, columns=everything):
+        cols = slice(*columns)
+        width = columns[1] - columns[0]
         increment = jnp.dot(
-            pert[...].reshape(2 * mm, 3 * kk), gain[l], preferred_element_type=F32
-        )
-        base = means[l][0:1][None] + root[None] * anom[l, pl.ds(2 * q, 2)].astype(F32)
-        result[l] = (base + increment.reshape(2, mm, half)).astype(BF16)
-        out_local(l).start()
-        out_remote(l).start()
+            pert[...].reshape(2 * mm, 3 * kk), gain[l, :, cols], preferred_element_type=F32
+        )
+        base = means[l, 0:1, cols][None] + root[None] * anom[l, pl.ds(2 * q, 2), :, cols].astype(F32)
+        result[l, :, :, cols] = (base + increment.reshape(2, mm, width)).astype(BF16)
+        for p in range(columns[0] // piece, columns[1] // piece):
+            out_remote(l, p).start()
+            out_local(l, p).start()
 
     def side_gain(l, carry):
         gain_rows(l, (0, 2))
         return carry
 
     lax.fori_loop(0, 2, side_gain, 0)
+    own_window(2, (0, 1, 2))
+
+    @pl.when(low_end)
+    def _():
+        relay(1)
+        make_pert()
+
+    @pl.when(high_end)
+    def _():
+        relay(0)
+        make_pert()
+
+    own_window(3, (0, 1, 2))
     for side in (0, 1):
 
         @pl.when(has_side[side])
@@ -551,13 +659,14 @@
             side_pert(1 - side).wait_recv()
             pert_forward(side, c).start()
 
-    ready = min(READY, nl)
+    root = scale[0:1, 0:1]
+    ready = min(READY, nl - 1)
 
     def ahead(l, carry):
         own_window(l, (0, 1, 2))
         return carry
 
-    lax.fori_loop(2, ready, ahead, 0)
+    lax.fori_loop(4, ready, ahead, 0)
     sib_pert(1 - c).wait_recv()
     for side in (0, 1):
 
@@ -576,14 +685,19 @@
         finish_variable(l)
         return carry
 
-    lax.fori_loop(ready, nl, one_variable, 0)
+    lax.fori_loop(ready, nl - 1, one_variable, 0)
+    for p in range(PIECES):
+        columns = (p * piece, (p + 1) * piece)
+        own_window(nl - 1, (0, 1, 2), columns)
+        finish_variable(nl - 1, columns)
 
     def finish(l, carry):
-        for j in range(1, nm):
-            bulk(l, j).wait_send()
-        out_local(l).wait()
-        out_remote(l).wait_send()
-        out_from(l).wait_recv()
+        for p in range(PIECES):
+            for j in range(1, nm):
+                bulk(l * PIECES + p, j).wait_send()
+            out_local(l, p).wait()
+            out_remote(l, p).wait_send()
+            out_from(l, p).wait_recv()
         return carry
 
     lax.fori_loop(0, nl, finish, 0)
@@ -593,8 +707,12 @@
         square_copy(j, me).wait_send()
     for g in range(1, ng):
         obs_copy(2 * g, me).wait_send()
-    for g in range(ng):
-        obs_forward(1, cross(g), g).wait_send()
+    obs_forward(1, me, 0, 0, kk).wait_send()
+    for g in range(1, ng):
+        for i in range(1, nd):
+            obs_swap(g, i, d).wait_send()
+        for h in range(nd):
+            obs_forward(1, cross(g), g, h, hk).wait_send()
     sib_pert(c).wait_send()
     for way in (0, 1):
 
@@ -606,9 +724,12 @@
 
         @pl.when(has_side[side])
         def _():
-            for g in range(ng):
-                side_obs(side, cross(g), g).wait_send()
-                obs_forward(2 * side, cross(g), g).wait_send()
+            side_obs(side, me, 0, 0, kk).wait_send()
+            obs_forward(2 * side, me, 0, 0, kk).wait_send()
+            for g in range(1, ng):
+                for h in range(nd):
+                    side_obs(side, cross(g), g, h, hk).wait_send()
+                obs_forward(2 * side, cross(g), g, 0, kk).wait_send()
             side_pert(side).wait_send()
             pert_forward(side, c).wait_send()
             stat_copy(side).wait_send()
@@ -662,10 +783,12 @@
                 pltpu.VMEM((nl, 8, half), F32),
                 pltpu.VMEM((nl, 3 * kk, half), BF16),
                 pltpu.VMEM((nl, 2, mm, half), BF16),
+                pltpu.VMEM((1, 128), F32),
+                pltpu.SemaphoreType.REGULAR((2,)),
                 dma((4,)),
                 dma((3,)),
-                dma((nl, nm)),
-                dma((nl, nm)),
+                dma((nl * PIECES, nm)),
+                dma((nl * PIECES, nm)),
                 dma((nd,)),
                 dma((nd,)),
                 dma((nm,)),
@@ -674,8 +797,10 @@
                 dma((nm,)),
                 dma((2,)),
                 dma((2,)),
-                dma((2, ng)),
-                dma((2, ng)),
+                dma((ng, nd)),
+                dma((ng, nd)),
+                dma((2, ng, nd)),
+                dma((2, ng, nd)),
                 dma((2,)),
                 dma((2,)),
                 dma((2,)),
@@ -686,11 +811,11 @@
                 dma((2,)),
                 dma((2,)),
                 dma((2,)),
-                dma((3, ng)),
-                dma((3, ng)),
-                dma((nl,)),
-                dma((nl,)),
-                dma((nl,)),
+                dma((3, ng, nd)),
+                dma((3, ng, nd)),
+                dma((nl, PIECES)),
+                dma((nl, PIECES)),
+                dma((nl, PIECES)),
             ],
             compiler_params=pltpu.CompilerParams(
                 collective_id=0, has_side_effects=True, vmem_limit_bytes=56 * 1024 * 1024

time: 44.5 us -> 43.1 us (0.969)
  Pallas kernels: 40.9 us -> 39.6 us
    pallas_call x1, Pallas kernels: 40.9 us -> 39.6 us  [shards(): pl.pallas_call(functools.partial(kernel, (nr, nd, nm, nl, mm, tt, kk)), o...]
where the time goes in v2:
time: 43.1 us; the launch traced here: 43 us
  Pallas kernels  39.6 us (92%)
  between operations  2.34 us (5%)
  local copies, waits for them, and re-layouts  1.08 us (3%)
    pallas_call x1, Pallas kernels, shards(): pl.pallas_call(functools.partial(kernel, (nr, nd, nm, nl, mm, tt, kk)), o...  39.6 us
    unnamed x1, local copies, waits for them, and re-layouts  1.08 us

profile of v2, /device:TPU:0, one launch (start us, length us, event | category | flops | bytes accessed | tf_op | source)
XLA Modules:
  0.0 43.0 jit_solution(14856910019199926181)
XLA Ops:
  0.6 39.6 %shard_map.77 = (bf16[7,96,1024]{2,1,0:T(8,128)(2,1)S(1)}, f32[1,1]{1,0:T(1,128)}) custom-call(f32[7]{0:T(128)} %weights_hbm.1, bf16[7,96,1024]{2,1,0:T(8,128)(2,1)} %ensemble.1, s32[1,512]{1,0:T(1,128)} %bitcast.4, f32[1,512]{1,0:T(1,128)} %bitcast.5, f32[1,512]{1,0:T(1,128)} %bitcast.6, f32[96,512]{1,0:T(8,128)} %noise.1), custom_call_target="tpu_custom_call" | custom-call | tf_op jit(solution)/shard_map/pallas_call | solution.py:755
  40.2 1.1 %copy.12 = bf16[7,96,1024]{2,1,0:T(8,128)(2,1)} copy(bf16[7,96,1024]{2,1,0:T(8,128)(2,1)S(1)} %shard_map.78) | data formatting | bytes 2752512
  (1 shorter events, 0.0 us)

commit v3 on v2

--- a/solution.py
+++ b/solution.py
@@ -8,7 +8,7 @@
 from jax.sharding import PartitionSpec as P
 
 RADIUS = 1024
-LEAD = 3
+LEAD = 4
 READY = 5
 PIECES = 2
 F32 = jnp.float32
@@ -49,6 +49,7 @@
     gain,
     result,
     scale,
+    infl_v,
     answer,
     small_sem,
     local_sem,
@@ -148,32 +149,37 @@
     pl.semaphore_wait(barrier, nm - 1 + d + (r > 0).astype(jnp.int32))
 
     piece = half // PIECES
-    units = nl * PIECES
-
-    def bulk(u, j):
-        to = (me + j) % nm
-        l, at = u // PIECES, (u % PIECES) * piece
-        return rdma(
-            ensemble.at[l, :, pl.ds(pl.multiple_of((to % 2) * half + at, 128), piece)],
-            gathered.at[l, me, :, pl.ds(pl.multiple_of(at, 128), piece)],
-            send_e.at[u, j],
-            recv_e.at[u, me],
-            dev(member=to),
-        )
-
-    def bulk_from(u, j):
-        slot = (me + j) % nm
-        l, at = u // PIECES, (u % PIECES) * piece
-        block = gathered.at[l, slot, :, pl.ds(pl.multiple_of(at, 128), piece)]
-        return rdma(block, block, send_e.at[u, j], recv_e.at[u, slot], dev(member=slot))
-
-    def send_bulk(u, carry):
-        for j in range(1, nm):
-            bulk(u, j).start()
-        return carry
-
-    lead = min(LEAD, units)
-    lax.fori_loop(0, lead, send_bulk, 0)
+    small = half // 4
+    last = nl - 1
+    units = (
+        [(0, 0, half)]
+        + [(1, p * small, small) for p in range(4)]
+        + [(l, 0, half) for l in range(2, last)]
+        + [(last, p * piece, piece) for p in range(PIECES)]
+    )
+
+    def arrival(l, lo):
+        return recv_e.at[l + lo // piece] if isinstance(l, int) and l == last else recv_e.at[l]
+
+    def send_bulk(chosen):
+        for l, lo, width in chosen:
+            for j in range(1, nm):
+                to = (me + j) % nm
+                rdma(
+                    ensemble.at[
+                        l, :, pl.ds(pl.multiple_of((to % 2) * half + lo, 128), width)
+                    ],
+                    gathered.at[l, me, :, pl.ds(lo, width)],
+                    send_e.at[0],
+                    arrival(l, lo),
+                    dev(member=to),
+                ).start()
+
+    def wait_bulk(l, lo, width):
+        block = gathered.at[l, pl.ds(0, nm - 1), :, pl.ds(lo, width)]
+        rdma(block, block, send_e.at[0], arrival(l, lo), dev(member=sib)).wait_recv()
+
+    send_bulk(units[:LEAD])
     for i in range(1, nd):
 
         @pl.when(d >= i)
@@ -346,7 +352,7 @@
     for g in range(1, ng):
         obs_copy(2 * g, me).start()
     obs_forward(1, me, 0, 0, kk).start()
-    lax.fori_loop(lead, units, send_bulk, 0)
+    send_bulk(units[LEAD:])
     for side in (0, 1):
 
         @pl.when(has_side[side])
@@ -470,11 +476,16 @@
             cov = jnp.dot(obs_t[rows_of], right, preferred_element_type=F32)
             gain[l, rows_of, cols] = (cov * taper[rows_of, cols]).astype(BF16)
 
+    def gain_part(l, h):
+        at = pl.ds(pl.multiple_of(kk + h * hk, 128), hk)
+        cov = jnp.dot(
+            obs_t[at], anom[l].reshape(members, half), preferred_element_type=F32
+        )
+        gain[l, at] = (cov * taper[at]).astype(BF16)
+
     def center(l, columns=everything):
         cols = slice(*columns)
-        for u in range(columns[0] // piece, columns[1] // piece):
-            for j in range(1, nm):
-                bulk_from(l * PIECES + u, j).wait_recv()
+        wait_bulk(l, columns[0], columns[1] - columns[0])
         raw = gathered[l, :, :, cols].astype(F32)
         mean = jnp.sum(jnp.sum(raw, axis=0), axis=0, keepdims=True) / members
         means[l, :, cols] = jnp.broadcast_to(mean, (8, columns[1] - columns[0]))
@@ -509,7 +520,8 @@
             grand = grand + everyone[i : i + 1]
         inflation = grand[0:1, 0:1] / grand[0:1, 1:2]
         root = jnp.sqrt(inflation)
-        infl_out[...] = inflation
+        infl_v[...] = inflation
+        pltpu.make_async_copy(infl_v, infl_out, small_sem.at[4]).start()
         scale[...] = jnp.broadcast_to(root, (1, 128))
         factor = inflation / (inflation * spread + error)
         local_noise.wait()
@@ -542,18 +554,22 @@
     transpose_part(1, d, hk)
     local_half.wait()
     center(0)
+    gain_part(0, d)
     for i in range(1, nd):
         h = (d + i) % nd
         for g in range(1, ng):
             obs_swap(g, i, h).wait_recv()
             hand_part(g, h)
     center(1)
+    gain_part(1, d)
     for i in range(1, nd):
         h = (d + i) % nd
         for g in range(1, ng):
             obs_forward(1, cross_sib(g), g, h, hk).wait_recv()
         transpose_part(1, h, hk)
-    gain_rows(0, (1,))
+        gain_part(0, h)
+        gain_part(1, h)
+    own_window(2, (1,))
 
     for side in (0, 1):
 
@@ -566,7 +582,6 @@
                     side_from(side, cross(g), g, h, hk).wait_recv()
                 obs_forward(2 * side, cross(g), g, 0, kk).start()
 
-    gain_rows(1, (1,))
 
     @pl.when(mid_low)
     def _():
@@ -594,33 +609,23 @@
 
         transpose_part(2 * side, 0, kk)
 
-    def out_block(l, which, p):
-        at = which * half + p * piece
-        return out.at[l, :, pl.ds(pl.multiple_of(at, 128), piece)]
-
-    def out_piece(l, which, p):
-        return result.at[l, which, :, p * piece : (p + 1) * piece]
-
-    def out_local(l, p):
-        return pltpu.make_async_copy(out_piece(l, c, p), out_block(l, c, p), own_out.at[l, p])
-
-    def out_remote(l, p):
-        return rdma(
-            out_piece(l, 1 - c, p),
-            out_block(l, c, p),
-            send_out.at[l, p],
-            recv_out.at[l, p],
+    def out_block(l, which, columns):
+        lo, width = columns[0], columns[1] - columns[0]
+        return out.at[l, :, pl.ds(pl.multiple_of(which * half + lo, 128), width)]
+
+    def out_copies(l, columns):
+        cols = slice(*columns)
+        there = rdma(
+            result.at[l, 1 - c, :, cols],
+            out_block(l, c, columns),
+            send_out.at[0],
+            recv_out.at[0],
             dev(member=sib),
         )
-
-    def out_from(l, p):
-        return rdma(
-            out_piece(l, 1 - c, p),
-            out_block(l, 1 - c, p),
-            send_out.at[l, p],
-            recv_out.at[l, p],
-            dev(member=sib),
-        )
+        here = pltpu.make_async_copy(
+            result.at[l, c, :, cols], out_block(l, c, columns), own_out.at[0]
+        )
+        return there, here
 
     def finish_variable(l, columns=everything):
         cols = slice(*columns)
@@ -630,16 +635,14 @@
         )
         base = means[l, 0:1, cols][None] + root[None] * anom[l, pl.ds(2 * q, 2), :, cols].astype(F32)
         result[l, :, :, cols] = (base + increment.reshape(2, mm, width)).astype(BF16)
-        for p in range(columns[0] // piece, columns[1] // piece):
-            out_remote(l, p).start()
-            out_local(l, p).start()
+        for copy in out_copies(l, columns):
+            copy.start()
 
     def side_gain(l, carry):
         gain_rows(l, (0, 2))
         return carry
 
-    lax.fori_loop(0, 2, side_gain, 0)
-    own_window(2, (0, 1, 2))
+    lax.fori_loop(0, 3, side_gain, 0)
 
     @pl.when(low_end)
     def _():
@@ -660,7 +663,7 @@
             pert_forward(side, c).start()
 
     root = scale[0:1, 0:1]
-    ready = min(READY, nl - 1)
+    ready = min(READY, last)
 
     def ahead(l, carry):
         own_window(l, (0, 1, 2))
@@ -685,22 +688,21 @@
         finish_variable(l)
         return carry
 
-    lax.fori_loop(ready, nl - 1, one_variable, 0)
+    lax.fori_loop(ready, last, one_variable, 0)
     for p in range(PIECES):
         columns = (p * piece, (p + 1) * piece)
-        own_window(nl - 1, (0, 1, 2), columns)
-        finish_variable(nl - 1, columns)
-
-    def finish(l, carry):
-        for p in range(PIECES):
-            for j in range(1, nm):
-                bulk(l * PIECES + p, j).wait_send()
-            out_local(l, p).wait()
-            out_remote(l, p).wait_send()
-            out_from(l, p).wait_recv()
-        return carry
-
-    lax.fori_loop(0, nl, finish, 0)
+        own_window(last, (0, 1, 2), columns)
+        finish_variable(last, columns)
+
+    sent = gathered.at[:, pl.ds(0, nm - 1)]
+    rdma(sent, sent, send_e.at[0], recv_e.at[0], dev(member=sib)).wait_send()
+    mine = out.at[:, :, pl.ds(pl.multiple_of(c * half, 128), half)]
+    other = out.at[:, :, pl.ds(pl.multiple_of((1 - c) * half, 128), half)]
+    pltpu.make_async_copy(mine, mine, own_out.at[0]).wait()
+    theirs = rdma(other, other, send_out.at[0], recv_out.at[0], dev(member=sib))
+    theirs.wait_send()
+    theirs.wait_recv()
+    pltpu.make_async_copy(infl_v, infl_out, small_sem.at[4]).wait()
     for i in range(1, nd):
         part_copy(i).wait_send()
     for j in range(1, nm):
@@ -759,7 +761,7 @@
                 jax.ShapeDtypeStruct((1, 1), F32),
             ),
             in_specs=[anywhere] * 6,
-            out_specs=(vmem, vmem),
+            out_specs=(vmem, anywhere),
             scratch_shapes=[
                 pltpu.SMEM((nl,), F32),
                 pltpu.VMEM((1, kk), jnp.int32),
@@ -784,11 +786,12 @@
                 pltpu.VMEM((nl, 3 * kk, half), BF16),
                 pltpu.VMEM((nl, 2, mm, half), BF16),
                 pltpu.VMEM((1, 128), F32),
+                pltpu.VMEM((1, 1), F32),
                 pltpu.SemaphoreType.REGULAR((2,)),
-                dma((4,)),
+                dma((5,)),
                 dma((3,)),
-                dma((nl * PIECES, nm)),
-                dma((nl * PIECES, nm)),
+                dma((1,)),
+                dma((nl - 1 + PIECES,)),
                 dma((nd,)),
                 dma((nd,)),
                 dma((nm,)),
@@ -813,9 +816,9 @@
                 dma((2,)),
                 dma((3, ng, nd)),
                 dma((3, ng, nd)),
-                dma((nl, PIECES)),
-                dma((nl, PIECES)),
-                dma((nl, PIECES)),
+                dma((1,)),
+                dma((1,)),
+                dma((1,)),
             ],
             compiler_params=pltpu.CompilerParams(
                 collective_id=0, has_side_effects=True, vmem_limit_bytes=56 * 1024 * 1024

time: 43.1 us -> 41.4 us (0.961)
  Pallas kernels: 39.6 us -> 37.8 us
    pallas_call x1, Pallas kernels: 39.6 us -> 37.8 us  [shards(): pl.pallas_call(functools.partial(kernel, (nr, nd, nm, nl, mm, tt, kk)), o...]
where the time goes in v3:
time: 41.4 us; the launch traced here: 41.2 us
  Pallas kernels  37.8 us (91%)
  between operations  2.34 us (6%)
  local copies, waits for them, and re-layouts  1.08 us (3%)
    pallas_call x1, Pallas kernels, shards(): pl.pallas_call(functools.partial(kernel, (nr, nd, nm, nl, mm, tt, kk)), o...  37.8 us
    unnamed x1, local copies, waits for them, and re-layouts  1.08 us

profile of v3, /device:TPU:0, one launch (start us, length us, event | category | flops | bytes accessed | tf_op | source)
XLA Modules:
  0.0 41.2 jit_solution(12958169120872641353)
XLA Ops:
  0.6 37.8 %shard_map.77 = (bf16[7,96,1024]{2,1,0:T(8,128)(2,1)S(1)}, f32[1,1]{1,0:T(1,128)}) custom-call(f32[7]{0:T(128)} %weights_hbm.1, bf16[7,96,1024]{2,1,0:T(8,128)(2,1)} %ensemble.1, s32[1,512]{1,0:T(1,128)} %bitcast.4, f32[1,512]{1,0:T(1,128)} %bitcast.5, f32[1,512]{1,0:T(1,128)} %bitcast.6, f32[96,512]{1,0:T(8,128)} %noise.1), custom_call_target="tpu_custom_call" | custom-call | tf_op jit(solution)/shard_map/pallas_call | solution.py:757
  38.4 1.1 %copy.12 = bf16[7,96,1024]{2,1,0:T(8,128)(2,1)} copy(bf16[7,96,1024]{2,1,0:T(8,128)(2,1)S(1)} %shard_map.78) | data formatting | bytes 2752512
  (1 shorter events, 0.0 us)

commit v4 on v3

--- a/solution.py
+++ b/solution.py
@@ -9,7 +9,7 @@
 
 RADIUS = 1024
 LEAD = 4
-READY = 5
+READY = 4
 PIECES = 2
 F32 = jnp.float32
 BF16 = jnp.bfloat16
@@ -69,7 +69,6 @@
     recv_z,
     send_st,
     recv_st,
-    send_pos,
     recv_pos,
     send_ps,
     recv_ps,
@@ -223,11 +222,13 @@
 
     def part_copy(i):
         to = (d + i) % nd
-        return rdma(part, part_in.at[d], send_p.at[i], recv_p.at[d], dev(depth=to))
+        return rdma(part, part_in.at[d], send_p.at[i - 1], recv_p.at[i - 1], dev(depth=to))
 
     def part_from(i):
         frm = (d + i) % nd
-        return rdma(part, part_in.at[frm], send_p.at[i], recv_p.at[frm], dev(depth=frm))
+        return rdma(
+            part, part_in.at[frm], send_p.at[i - 1], recv_p.at[nd - i - 1], dev(depth=frm)
+        )
 
     @pl.when(d < nd - 1)
     def _():
@@ -242,7 +243,7 @@
         return rdma(
             pos.at[1],
             pos.at[2 - 2 * side],
-            send_pos.at[side],
+            send_st.at[side],
             recv_pos.at[1 - side],
             dev(region=r + (2 * side - 1)),
         )
@@ -251,7 +252,7 @@
         return rdma(
             pos.at[1],
             pos.at[2 * side],
-            send_pos.at[side],
+            send_st.at[side],
             recv_pos.at[side],
             dev(region=r + (2 * side - 1)),
         )
@@ -294,76 +295,88 @@
     squares[me] = jnp.where(qrow == 0, own_sum, own_square)
     obs[me, :, kk : 2 * kk] = spread_in.astype(BF16)
 
-    def square_copy(j, slot):
-        return rdma(
-            squares.at[slot],
-            squares.at[slot],
-            send_q.at[j],
-            recv_q.at[slot],
+    def square_copy(j):
+        return rdma(
+            squares.at[me],
+            squares.at[me],
+            send_q.at[0],
+            recv_q.at[0],
             dev(member=(me + j) % nm),
         )
+
+    square_rest = squares.at[pl.ds(0, nm - 1)]
+    square_all = rdma(square_rest, square_rest, send_q.at[0], recv_q.at[0], dev(member=sib))
 
     hk = kk // nd
 
     def obs_at(slot, w, h, width):
         return obs.at[slot, :, pl.ds(pl.multiple_of(w * kk + h * hk, 128), width)]
 
-    def obs_copy(j, slot):
-        block = obs_at(slot, 1, d, hk)
-        return rdma(block, block, send_o.at[j], recv_o.at[slot], dev(member=(me + j) % nm))
-
-    def obs_swap(g, i, h):
+    def obs_copy(g):
+        block = obs_at(me, 1, d, hk)
+        return rdma(
+            block, block, send_o.at[g - 1], recv_o.at[g - 1], dev(member=(me + 2 * g) % nm)
+        )
+
+    def obs_from(g):
+        block = obs_at(cross(g), 1, d, hk)
+        return rdma(block, block, send_o.at[g - 1], recv_o.at[ng - g - 1], dev(member=sib))
+
+    def obs_swap(g, i):
+        block = obs_at(cross(g), 1, d, hk)
+        return rdma(
+            block, block, send_y.at[g - 1, i - 1], recv_y.at[g - 1, i - 1], dev(depth=(d + i) % nd)
+        )
+
+    def swap_from(g, i):
+        h = (d + i) % nd
         block = obs_at(cross(g), 1, h, hk)
-        return rdma(block, block, send_y.at[g, i], recv_y.at[g, h], dev(depth=(d + i) % nd))
-
-    def side_obs(side, slot, pair, h, width):
+        return rdma(
+            block, block, send_y.at[g - 1, i - 1], recv_y.at[g - 1, nd - i - 1], dev(depth=h)
+        )
+
+    def side_obs(side, slot, h, width):
         return rdma(
             obs_at(slot, 1, h, width),
             obs_at(slot, 2 if side == 0 else 0, h, width),
-            send_z.at[side, pair, h],
-            recv_z.at[1 - side, pair, h],
+            send_z.at[side],
+            recv_z.at[1 - side],
             dev(region=r + (2 * side - 1)),
         )
 
-    def side_from(side, slot, pair, h, width):
-        block = obs_at(slot, 2 * side, h, width)
-        return rdma(
-            block,
-            block,
-            send_z.at[side, pair, h],
-            recv_z.at[side, pair, h],
-            dev(region=r + (2 * side - 1)),
-        )
-
-    def obs_forward(w, slot, pair, h, width):
+    def side_all(side):
+        block = obs.at[pl.ds(0, ng), :, pl.ds(kk, kk)]
+        return rdma(
+            block, block, send_z.at[side], recv_z.at[side], dev(region=r + (2 * side - 1))
+        )
+
+    def obs_forward(w, slot, h, width, number):
         block = obs_at(slot, w, h, width)
-        return rdma(
-            block, block, send_f.at[w, pair, h], recv_f.at[w, pair, h], dev(member=sib)
-        )
+        return rdma(block, block, send_f.at[w], recv_f.at[number], dev(member=sib))
+
+    def forward_all(w, wide, number):
+        block = obs.at[pl.ds(0, wide[0]), :, pl.ds(0, wide[1])]
+        return rdma(block, block, send_f.at[w], recv_f.at[number], dev(member=sib))
 
     def cross(g):
         return 2 * ((q + g) % ng) + c
 
-    def cross_sib(g):
-        return 2 * ((q + g) % ng) + (1 - c)
-
     for j in range(1, nm):
-        square_copy(j, me).start()
+        square_copy(j).start()
     for g in range(1, ng):
-        obs_copy(2 * g, me).start()
-    obs_forward(1, me, 0, 0, kk).start()
+        obs_copy(g).start()
+    obs_forward(1, me, 0, kk, 0).start()
     send_bulk(units[LEAD:])
     for side in (0, 1):
 
         @pl.when(has_side[side])
         def _():
-            side_obs(side, me, 0, 0, kk).start()
+            side_obs(side, me, 0, kk).start()
             pos_from(side).wait_recv()
 
         make_taper(2 * side)
 
-    for j in range(1, nm):
-        square_copy(j, (me + j) % nm).wait_recv()
+    square_all.wait_recv()
     moments = [squares[j] for j in range(nm)]
     obs_mean = sum(m[0:1] for m in moments) / members
     deviation = predicted - obs_mean
@@ -443,20 +456,21 @@
         def _():
             stat_copy(side).start()
 
-    def hand_part(g, h):
+    def hand_part(g, i):
+        h = (d + i) % nd
         for side in (0, 1):
 
             @pl.when(has_side[side])
             def _():
-                side_obs(side, cross(g), g, h, hk).start()
-
-        obs_forward(1, cross(g), g, h, hk).start()
+                side_obs(side, cross(g), h, hk).start()
+
+        obs_forward(1, cross(g), h, hk, i).start()
 
     for g in range(1, ng):
-        obs_copy(2 * g, cross(g)).wait_recv()
+        obs_from(g).wait_recv()
         for i in range(1, nd):
-            obs_swap(g, i, d).start()
-        hand_part(g, d)
+            obs_swap(g, i).start()
+        hand_part(g, 0)
 
     def transpose_part(w, h, width):
         at = pl.multiple_of(h * hk, 128)
@@ -548,24 +562,31 @@
     def _():
         relay(1)
 
-    obs_forward(1, sib, 0, 0, kk).wait_recv()
-    for g in range(1, ng):
-        obs_forward(1, cross_sib(g), g, d, hk).wait_recv()
+    forward_all(1, (1, kk + (ng - 1) * hk), 0).wait_recv()
     transpose_part(1, d, hk)
     local_half.wait()
     center(0)
     gain_part(0, d)
     for i in range(1, nd):
-        h = (d + i) % nd
         for g in range(1, ng):
-            obs_swap(g, i, h).wait_recv()
-            hand_part(g, h)
+            swap_from(g, i).wait_recv()
+            hand_part(g, i)
     center(1)
     gain_part(1, d)
+
+    @pl.when(mid_low)
+    def _():
+        relay(1)
+        make_pert()
+
+    @pl.when(mid_high)
+    def _():
+        relay(0)
+        make_pert()
+
     for i in range(1, nd):
         h = (d + i) % nd
-        for g in range(1, ng):
-            obs_forward(1, cross_sib(g), g, h, hk).wait_recv()
+        forward_all(1, (1, (ng - 1) * hk), i).wait_recv()
         transpose_part(1, h, hk)
         gain_part(0, h)
         gain_part(1, h)
@@ -575,20 +596,17 @@
 
         @pl.when(has_side[side])
         def _():
-            side_from(side, me, 0, 0, kk).wait_recv()
-            obs_forward(2 * side, me, 0, 0, kk).start()
-            for g in range(1, ng):
-                for h in range(nd):
-                    side_from(side, cross(g), g, h, hk).wait_recv()
-                obs_forward(2 * side, cross(g), g, 0, kk).start()
-
-
-    @pl.when(mid_low)
+            side_all(side).wait_recv()
+            for g in range(ng):
+                obs_forward(2 * side, cross(g), 0, kk, nd + side).start()
+
+
+    @pl.when(low_end)
     def _():
         relay(1)
         make_pert()
 
-    @pl.when(mid_high)
+    @pl.when(high_end)
     def _():
         relay(0)
         make_pert()
@@ -604,8 +622,7 @@
                 recv_st.at[side],
                 dev(region=r + (2 * side - 1)),
             ).wait_recv()
-            for g in range(ng):
-                obs_forward(2 * side, cross_sib(g), g, 0, kk).wait_recv()
+            forward_all(2 * side, (ng, kk), nd + side).wait_recv()
 
         transpose_part(2 * side, 0, kk)
 
@@ -644,23 +661,14 @@
 
     lax.fori_loop(0, 3, side_gain, 0)
 
-    @pl.when(low_end)
-    def _():
-        relay(1)
-        make_pert()
-
-    @pl.when(high_end)
-    def _():
-        relay(0)
-        make_pert()
-
-    own_window(3, (0, 1, 2))
     for side in (0, 1):
 
         @pl.when(has_side[side])
         def _():
             side_pert(1 - side).wait_recv()
             pert_forward(side, c).start()
+
+    own_window(3, (0, 1, 2))
 
     root = scale[0:1, 0:1]
     ready = min(READY, last)
@@ -705,16 +713,12 @@
     pltpu.make_async_copy(infl_v, infl_out, small_sem.at[4]).wait()
     for i in range(1, nd):
         part_copy(i).wait_send()
-    for j in range(1, nm):
-        square_copy(j, me).wait_send()
+    square_all.wait_send()
     for g in range(1, ng):
-        obs_copy(2 * g, me).wait_send()
-    obs_forward(1, me, 0, 0, kk).wait_send()
-    for g in range(1, ng):
+        obs_copy(g).wait_send()
         for i in range(1, nd):
-            obs_swap(g, i, d).wait_send()
-        for h in range(nd):
-            obs_forward(1, cross(g), g, h, hk).wait_send()
+            obs_swap(g, i).wait_send()
+    forward_all(1, (ng, kk), 0).wait_send()
     sib_pert(c).wait_send()
     for way in (0, 1):
 
@@ -726,16 +730,14 @@
 
         @pl.when(has_side[side])
         def _():
-            side_obs(side, me, 0, 0, kk).wait_send()
-            obs_forward(2 * side, me, 0, 0, kk).wait_send()
-            for g in range(1, ng):
-                for h in range(nd):
-                    side_obs(side, cross(g), g, h, hk).wait_send()
-                obs_forward(2 * side, cross(g), g, 0, kk).wait_send()
+            side_all(side).wait_send()
+            forward_all(2 * side, (ng, kk), nd + side).wait_send()
             side_pert(side).wait_send()
             pert_forward(side, c).wait_send()
-            stat_copy(side).wait_send()
-            pos_copy(side).wait_send()
+            both = stats.at[pl.ds(0, 2)]
+            rdma(
+                both, both, send_st.at[side], recv_st.at[side], dev(region=r + (2 * side - 1))
+            ).wait_send()
 
 
 def hand_on(block, out):
@@ -792,30 +794,29 @@
                 dma((3,)),
                 dma((1,)),
                 dma((nl - 1 + PIECES,)),
-                dma((nd,)),
-                dma((nd,)),
-                dma((nm,)),
-                dma((nm,)),
-                dma((nm,)),
-                dma((nm,)),
-                dma((2,)),
-                dma((2,)),
-                dma((ng, nd)),
-                dma((ng, nd)),
-                dma((2, ng, nd)),
-                dma((2, ng, nd)),
-                dma((2,)),
-                dma((2,)),
-                dma((2,)),
-                dma((2,)),
+                dma((nd - 1,)),
+                dma((nd - 1,)),
                 dma((1,)),
                 dma((1,)),
-                dma((2,)),
-                dma((2,)),
-                dma((2,)),
-                dma((2,)),
-                dma((3, ng, nd)),
-                dma((3, ng, nd)),
+                dma((ng - 1,)),
+                dma((ng - 1,)),
+                dma((2,)),
+                dma((2,)),
+                dma((ng - 1, nd - 1)),
+                dma((ng - 1, nd - 1)),
+                dma((2,)),
+                dma((2,)),
+                dma((2,)),
+                dma((2,)),
+                dma((2,)),
+                dma((1,)),
+                dma((1,)),
+                dma((2,)),
+                dma((2,)),
+                dma((2,)),
+                dma((2,)),
+                dma((3,)),
+                dma((nd + 2,)),
                 dma((1,)),
                 dma((1,)),
                 dma((1,)),

time: 41.4 us -> 40.9 us (0.988)
  Pallas kernels: 37.8 us -> 37.3 us
    pallas_call x1, Pallas kernels: 37.8 us -> 37.3 us  [shards(): pl.pallas_call(functools.partial(kernel, (nr, nd, nm, nl, mm, tt, kk)), o...]
where the time goes in v4:
time: 40.9 us; the launch traced here: 40.7 us
  Pallas kernels  37.3 us (91%)
  between operations  2.34 us (6%)
  local copies, waits for them, and re-layouts  1.08 us (3%)
    pallas_call x1, Pallas kernels, shards(): pl.pallas_call(functools.partial(kernel, (nr, nd, nm, nl, mm, tt, kk)), o...  37.3 us
    unnamed x1, local copies, waits for them, and re-layouts  1.08 us

profile of v4, /device:TPU:0, one launch (start us, length us, event | category | flops | bytes accessed | tf_op | source)
XLA Modules:
  0.0 40.7 jit_solution(17957624342523799102)
XLA Ops:
  0.6 37.3 %shard_map.77 = (bf16[7,96,1024]{2,1,0:T(8,128)(2,1)S(1)}, f32[1,1]{1,0:T(1,128)}) custom-call(f32[7]{0:T(128)} %weights_hbm.1, bf16[7,96,1024]{2,1,0:T(8,128)(2,1)} %ensemble.1, s32[1,512]{1,0:T(1,128)} %bitcast.4, f32[1,512]{1,0:T(1,128)} %bitcast.5, f32[1,512]{1,0:T(1,128)} %bitcast.6, f32[96,512]{1,0:T(8,128)} %noise.1), custom_call_target="tpu_custom_call" | custom-call | tf_op jit(solution)/shard_map/pallas_call | solution.py:759
  38.0 1.1 %copy.12 = bf16[7,96,1024]{2,1,0:T(8,128)(2,1)} copy(bf16[7,96,1024]{2,1,0:T(8,128)(2,1)S(1)} %shard_map.78) | data formatting | bytes 2752512
  (1 shorter events, 0.0 us)

commit v5 on v4

--- a/solution.py
+++ b/solution.py
@@ -8,7 +8,7 @@
 from jax.sharding import PartitionSpec as P
 
 RADIUS = 1024
-LEAD = 4
+LEAD = 2
 READY = 4
 PIECES = 2
 F32 = jnp.float32
@@ -49,7 +49,6 @@
     gain,
     result,
     scale,
-    infl_v,
     answer,
     small_sem,
     local_sem,
@@ -152,7 +151,7 @@
     last = nl - 1
     units = (
         [(0, 0, half)]
-        + [(1, p * small, small) for p in range(4)]
+        + [(1, p * piece, piece) for p in range(PIECES)]
         + [(l, 0, half) for l in range(2, last)]
         + [(last, p * piece, piece) for p in range(PIECES)]
     )
@@ -162,8 +161,7 @@
 
     def send_bulk(chosen):
         for l, lo, width in chosen:
-            for j in range(1, nm):
-                to = (me + j) % nm
+            for to in [(me + 2 * g) % nm for g in range(1, ng)] + [(sib + 2 * g) % nm for g in range(ng)]:
                 rdma(
                     ensemble.at[
                         l, :, pl.ds(pl.multiple_of((to % 2) * half + lo, 128), width)
@@ -534,8 +532,7 @@
             grand = grand + everyone[i : i + 1]
         inflation = grand[0:1, 0:1] / grand[0:1, 1:2]
         root = jnp.sqrt(inflation)
-        infl_v[...] = inflation
-        pltpu.make_async_copy(infl_v, infl_out, small_sem.at[4]).start()
+        infl_out[...] = inflation
         scale[...] = jnp.broadcast_to(root, (1, 128))
         factor = inflation / (inflation * spread + error)
         local_noise.wait()
@@ -710,7 +707,6 @@
     theirs = rdma(other, other, send_out.at[0], recv_out.at[0], dev(member=sib))
     theirs.wait_send()
     theirs.wait_recv()
-    pltpu.make_async_copy(infl_v, infl_out, small_sem.at[4]).wait()
     for i in range(1, nd):
         part_copy(i).wait_send()
     square_all.wait_send()
@@ -760,10 +756,10 @@
             functools.partial(kernel, (nr, nd, nm, nl, mm, tt, kk)),
             out_shape=(
                 pltpu.VMEM((nl, mm, tt), BF16),
-                jax.ShapeDtypeStruct((1, 1), F32),
+                pltpu.VMEM((1, 1), F32),
             ),
             in_specs=[anywhere] * 6,
-            out_specs=(vmem, anywhere),
+            out_specs=(vmem, vmem),
             scratch_shapes=[
                 pltpu.SMEM((nl,), F32),
                 pltpu.VMEM((1, kk), jnp.int32),
@@ -788,9 +784,8 @@
                 pltpu.VMEM((nl, 3 * kk, half), BF16),
                 pltpu.VMEM((nl, 2, mm, half), BF16),
                 pltpu.VMEM((1, 128), F32),
-                pltpu.VMEM((1, 1), F32),
                 pltpu.SemaphoreType.REGULAR((2,)),
-                dma((5,)),
+                dma((4,)),
                 dma((3,)),
                 dma((1,)),
                 dma((nl - 1 + PIECES,)),

time: 40.9 us -> 40.4 us (0.988)
  between operations: 2.34 us -> 1.81 us
where the time goes in v5:
time: 40.4 us; the launch traced here: 40.2 us
  Pallas kernels  37.3 us (92%)
  between operations  1.81 us (4%)
  local copies, waits for them, and re-layouts  1.08 us (3%)
    pallas_call x1, Pallas kernels, shards(): pl.pallas_call(functools.partial(kernel, (nr, nd, nm, nl, mm, tt, kk)), o...  37.3 us
    unnamed x1, local copies, waits for them, and re-layouts  1.08 us

profile of v5, /device:TPU:0, one launch (start us, length us, event | category | flops | bytes accessed | tf_op | source)
XLA Modules:
  0.0 40.2 jit_solution(7606956286725475714)
XLA Ops:
  0.6 37.3 %shard_map.77 = (bf16[7,96,1024]{2,1,0:T(8,128)(2,1)S(1)}, f32[1,1]{1,0:T(1,128)S(1)}) custom-call(f32[7]{0:T(128)} %weights_hbm.1, bf16[7,96,1024]{2,1,0:T(8,128)(2,1)} %ensemble.1, s32[1,512]{1,0:T(1,128)} %bitcast.4, f32[1,512]{1,0:T(1,128)} %bitcast.5, f32[1,512]{1,0:T(1,128)} %bitcast.6, f32[96,512]{1,0:T(8,128)} %noise.1), custom_call_target="tpu_custom_call" | custom-call | tf_op jit(solution)/shard_map/pallas_call | solution.py:755
  38.0 1.1 %copy.12 = bf16[7,96,1024]{2,1,0:T(8,128)(2,1)} copy(bf16[7,96,1024]{2,1,0:T(8,128)(2,1)S(1)} %shard_map.78) | data formatting | bytes 2752512
  (1 shorter events, 0.0 us)

commit v6 on v5

--- a/solution.py
+++ b/solution.py
@@ -274,14 +274,6 @@
         def _():
             pos_copy(side).start()
 
-        @pl.when(jnp.logical_not(has_side[side]))
-        def _():
-            window = 0 if side == 0 else 2 * kk
-            obs[:, :, window : window + kk] = jnp.zeros((nm, mm, kk), BF16)
-            pert[:, :, window : window + kk] = jnp.zeros((2, mm, kk), BF16)
-            stats[2 * side] = jnp.zeros((8, kk), F32)
-            pos[2 * side] = jnp.zeros((8, kk), F32)
-
     predicted = whole(part[...])
     for i in range(1, nd):
         part_from(i).wait_recv()
@@ -305,38 +297,47 @@
     square_rest = squares.at[pl.ds(0, nm - 1)]
     square_all = rdma(square_rest, square_rest, send_q.at[0], recv_q.at[0], dev(member=sib))
 
-    hk = kk // nd
-
-    def obs_at(slot, w, h, width):
-        return obs.at[slot, :, pl.ds(pl.multiple_of(w * kk + h * hk, 128), width)]
-
-    def obs_copy(g):
-        block = obs_at(me, 1, d, hk)
+    first_part = kk // (2 * nd)
+    cuts = [0] + [first_part + (kk - first_part) * h // (nd - 1) for h in range(nd)]
+    parts = [(cuts[h], cuts[h + 1] - cuts[h]) for h in range(nd)]
+    whole_slot = (0, kk)
+
+    def by_depth(step, ahead=0):
+        for h in range(nd):
+
+            @pl.when(d == (h - ahead) % nd)
+            def _():
+                step(h)
+
+    def obs_at(slot, w, extent):
+        return obs.at[slot, :, pl.ds(w * kk + extent[0], extent[1])]
+
+    def obs_copy(g, h):
+        block = obs_at(me, 1, parts[h])
         return rdma(
             block, block, send_o.at[g - 1], recv_o.at[g - 1], dev(member=(me + 2 * g) % nm)
         )
 
-    def obs_from(g):
-        block = obs_at(cross(g), 1, d, hk)
+    def obs_from(g, h):
+        block = obs_at(cross(g), 1, parts[h])
         return rdma(block, block, send_o.at[g - 1], recv_o.at[ng - g - 1], dev(member=sib))
 
-    def obs_swap(g, i):
-        block = obs_at(cross(g), 1, d, hk)
+    def obs_swap(g, i, h):
+        block = obs_at(cross(g), 1, parts[h])
         return rdma(
             block, block, send_y.at[g - 1, i - 1], recv_y.at[g - 1, i - 1], dev(depth=(d + i) % nd)
         )
 
-    def swap_from(g, i):
-        h = (d + i) % nd
-        block = obs_at(cross(g), 1, h, hk)
+    def swap_from(g, i, h):
+        block = obs_at(cross(g), 1, parts[h])
         return rdma(
             block, block, send_y.at[g - 1, i - 1], recv_y.at[g - 1, nd - i - 1], dev(depth=h)
         )
 
-    def side_obs(side, slot, h, width):
-        return rdma(
-            obs_at(slot, 1, h, width),
-            obs_at(slot, 2 if side == 0 else 0, h, width),
+    def side_obs(side, slot, extent):
+        return rdma(
+            obs_at(slot, 1, extent),
+            obs_at(slot, 2 if side == 0 else 0, extent),
             send_z.at[side],
             recv_z.at[1 - side],
             dev(region=r + (2 * side - 1)),
@@ -348,8 +349,8 @@
             block, block, send_z.at[side], recv_z.at[side], dev(region=r + (2 * side - 1))
         )
 
-    def obs_forward(w, slot, h, width, number):
-        block = obs_at(slot, w, h, width)
+    def obs_forward(w, slot, extent, number):
+        block = obs_at(slot, w, extent)
         return rdma(block, block, send_f.at[w], recv_f.at[number], dev(member=sib))
 
     def forward_all(w, wide, number):
@@ -361,18 +362,16 @@
 
     for j in range(1, nm):
         square_copy(j).start()
-    for g in range(1, ng):
-        obs_copy(g).start()
-    obs_forward(1, me, 0, kk, 0).start()
+    by_depth(lambda h: [obs_copy(g, h).start() for g in range(1, ng)])
+    obs_forward(1, me, whole_slot, 0).start()
     send_bulk(units[LEAD:])
     for side in (0, 1):
 
         @pl.when(has_side[side])
         def _():
-            side_obs(side, me, 0, kk).start()
+            side_obs(side, me, whole_slot).start()
             pos_from(side).wait_recv()
-
-        make_taper(2 * side)
+            make_taper(2 * side)
 
     square_all.wait_recv()
     moments = [squares[j] for j in range(nm)]
@@ -454,50 +453,68 @@
         def _():
             stat_copy(side).start()
 
-    def hand_part(g, i):
-        h = (d + i) % nd
+    def hand_part(g, i, h):
         for side in (0, 1):
 
             @pl.when(has_side[side])
             def _():
-                side_obs(side, cross(g), h, hk).start()
-
-        obs_forward(1, cross(g), h, hk, i).start()
-
-    for g in range(1, ng):
-        obs_from(g).wait_recv()
-        for i in range(1, nd):
-            obs_swap(g, i).start()
-        hand_part(g, 0)
-
-    def transpose_part(w, h, width):
-        at = pl.multiple_of(h * hk, 128)
-        rows_of = pl.ds(pl.multiple_of(w * kk + at, 128), width)
-        shifts = stats[w, :, pl.ds(at, width)].T
+                side_obs(side, cross(g), parts[h]).start()
+
+        obs_forward(1, cross(g), parts[h], i).start()
+
+    def take_part(h):
+        for g in range(1, ng):
+            obs_from(g, h).wait_recv()
+            for i in range(1, nd):
+                obs_swap(g, i, h).start()
+            hand_part(g, 0, h)
+
+    by_depth(take_part)
+
+    def transpose_part(w, extent):
+        lo, width = extent
+        rows_of = pl.ds(w * kk + lo, width)
+        shifts = stats[w, :, lo : lo + width].T
         for g in range(nm):
             block = obs[g, :, rows_of].astype(F32).T + shifts[:, g : g + 1]
             obs_t[rows_of, g * mm : (g + 1) * mm] = block.astype(BF16)
 
     everything = (0, half)
+
+    middle = jnp.logical_and(has_side[0], has_side[1])
+    beside = jnp.where(has_side[0], 0, 2)
+
+    def by_place(step):
+        @pl.when(middle)
+        def _():
+            step((0, 2))
+
+        @pl.when(jnp.logical_not(middle))
+        def _():
+            step((beside,))
+
+    def span(w):
+        return pl.ds(w * kk if isinstance(w, int) else pl.multiple_of(w * kk, 128), kk)
 
     def gain_rows(l, windows, columns=everything):
         cols = slice(*columns)
         right = anom[l, :, :, cols].reshape(members, columns[1] - columns[0])
         for w in windows:
-            rows_of = slice(w * kk, (w + 1) * kk)
-            cov = jnp.dot(obs_t[rows_of], right, preferred_element_type=F32)
-            gain[l, rows_of, cols] = (cov * taper[rows_of, cols]).astype(BF16)
+            cov = jnp.dot(obs_t[span(w)], right, preferred_element_type=F32)
+            gain[l, span(w), cols] = (cov * taper[span(w), cols]).astype(BF16)
 
     def gain_part(l, h):
-        at = pl.ds(pl.multiple_of(kk + h * hk, 128), hk)
+        at = pl.ds(kk + parts[h][0], parts[h][1])
         cov = jnp.dot(
             obs_t[at], anom[l].reshape(members, half), preferred_element_type=F32
         )
         gain[l, at] = (cov * taper[at]).astype(BF16)
 
+    def wait_variable(l, columns=everything):
+        wait_bulk(l, columns[0], columns[1] - columns[0])
+
     def center(l, columns=everything):
         cols = slice(*columns)
-        wait_bulk(l, columns[0], columns[1] - columns[0])
         raw = gathered[l, :, :, cols].astype(F32)
         mean = jnp.sum(jnp.sum(raw, axis=0), axis=0, keepdims=True) / members
         means[l, :, cols] = jnp.broadcast_to(mean, (8, columns[1] - columns[0]))
@@ -559,17 +576,27 @@
     def _():
         relay(1)
 
-    forward_all(1, (1, kk + (ng - 1) * hk), 0).wait_recv()
-    transpose_part(1, d, hk)
     local_half.wait()
+    wait_variable(0)
     center(0)
-    gain_part(0, d)
+
+    def own_part(h):
+        forward_all(1, (1, kk + (ng - 1) * parts[h][1]), 0).wait_recv()
+        transpose_part(1, parts[h])
+        gain_part(0, h)
+
+    by_depth(own_part)
+
+    def swap_part(i, h):
+        for g in range(1, ng):
+            swap_from(g, i, h).wait_recv()
+            hand_part(g, i, h)
+
     for i in range(1, nd):
-        for g in range(1, ng):
-            swap_from(g, i).wait_recv()
-            hand_part(g, i)
+        by_depth(functools.partial(swap_part, i), i)
+    wait_variable(1)
     center(1)
-    gain_part(1, d)
+    by_depth(lambda h: gain_part(1, h))
 
     @pl.when(mid_low)
     def _():
@@ -581,12 +608,15 @@
         relay(0)
         make_pert()
 
-    for i in range(1, nd):
-        h = (d + i) % nd
-        forward_all(1, (1, (ng - 1) * hk), i).wait_recv()
-        transpose_part(1, h, hk)
+    def other_part(i, h):
+        forward_all(1, (1, (ng - 1) * parts[h][1]), i).wait_recv()
+        transpose_part(1, parts[h])
         gain_part(0, h)
         gain_part(1, h)
+
+    for i in range(1, nd):
+        by_depth(functools.partial(other_part, i), i)
+    wait_variable(2)
     own_window(2, (1,))
 
     for side in (0, 1):
@@ -595,7 +625,7 @@
         def _():
             side_all(side).wait_recv()
             for g in range(ng):
-                obs_forward(2 * side, cross(g), 0, kk, nd + side).start()
+                obs_forward(2 * side, cross(g), whole_slot, nd + side).start()
 
 
     @pl.when(low_end)
@@ -621,7 +651,7 @@
             ).wait_recv()
             forward_all(2 * side, (ng, kk), nd + side).wait_recv()
 
-        transpose_part(2 * side, 0, kk)
+            transpose_part(2 * side, whole_slot)
 
     def out_block(l, which, columns):
         lo, width = columns[0], columns[1] - columns[0]
@@ -641,23 +671,38 @@
         )
         return there, here
 
-    def finish_variable(l, columns=everything):
+    def finish_variable(l, sides, columns=everything):
         cols = slice(*columns)
         width = columns[1] - columns[0]
-        increment = jnp.dot(
-            pert[...].reshape(2 * mm, 3 * kk), gain[l, :, cols], preferred_element_type=F32
-        )
-        base = means[l, 0:1, cols][None] + root[None] * anom[l, pl.ds(2 * q, 2), :, cols].astype(F32)
+        if len(sides) == 2:
+            increment = jnp.dot(
+                pert[...].reshape(2 * mm, 3 * kk), gain[l, :, cols], preferred_element_type=F32
+            )
+        else:
+            increment = jnp.zeros((2 * mm, width), F32)
+            for w in (1,) + sides:
+                increment = increment + jnp.dot(
+                    pert[:, :, span(w)].reshape(2 * mm, kk),
+                    gain[l, span(w), cols],
+                    preferred_element_type=F32,
+                )
+        base = means[l, 0:1, cols][None] + scale[0:1, 0:1][None] * anom[
+            l, pl.ds(2 * q, 2), :, cols
+        ].astype(F32)
         result[l, :, :, cols] = (base + increment.reshape(2, mm, width)).astype(BF16)
+
+    def send_result(l, columns=everything):
         for copy in out_copies(l, columns):
             copy.start()
 
-    def side_gain(l, carry):
-        gain_rows(l, (0, 2))
-        return carry
-
-    lax.fori_loop(0, 3, side_gain, 0)
-
+    def early_gain(sides):
+        def step(l, carry):
+            gain_rows(l, sides)
+            return carry
+
+        lax.fori_loop(0, 3, step, 0)
+
+    by_place(early_gain)
     for side in (0, 1):
 
         @pl.when(has_side[side])
@@ -665,16 +710,14 @@
             side_pert(1 - side).wait_recv()
             pert_forward(side, c).start()
 
-    own_window(3, (0, 1, 2))
-
-    root = scale[0:1, 0:1]
     ready = min(READY, last)
 
     def ahead(l, carry):
-        own_window(l, (0, 1, 2))
+        wait_variable(l)
+        by_place(lambda sides: own_window(l, (1,) + sides))
         return carry
 
-    lax.fori_loop(4, ready, ahead, 0)
+    lax.fori_loop(3, ready, ahead, 0)
     sib_pert(1 - c).wait_recv()
     for side in (0, 1):
 
@@ -683,21 +726,29 @@
             pert_forward(side, 1 - c).wait_recv()
 
     def late_variable(l, carry):
-        finish_variable(l)
+        by_place(lambda sides: finish_variable(l, sides))
+        send_result(l)
         return carry
 
     lax.fori_loop(0, ready, late_variable, 0)
 
+    def whole_variable(l, columns=everything):
+        wait_variable(l, columns)
+
+        def step(sides):
+            own_window(l, (1,) + sides, columns)
+            finish_variable(l, sides, columns)
+
+        by_place(step)
+        send_result(l, columns)
+
     def one_variable(l, carry):
-        own_window(l, (0, 1, 2))
-        finish_variable(l)
+        whole_variable(l)
         return carry
 
     lax.fori_loop(ready, last, one_variable, 0)
     for p in range(PIECES):
-        columns = (p * piece, (p + 1) * piece)
-        own_window(last, (0, 1, 2), columns)
-        finish_variable(last, columns)
+        whole_variable(last, (p * piece, (p + 1) * piece))
 
     sent = gathered.at[:, pl.ds(0, nm - 1)]
     rdma(sent, sent, send_e.at[0], recv_e.at[0], dev(member=sib)).wait_send()
@@ -710,10 +761,13 @@
     for i in range(1, nd):
         part_copy(i).wait_send()
     square_all.wait_send()
-    for g in range(1, ng):
-        obs_copy(g).wait_send()
-        for i in range(1, nd):
-            obs_swap(g, i).wait_send()
+    def parts_sent(h):
+        for g in range(1, ng):
+            obs_copy(g, h).wait_send()
+            for i in range(1, nd):
+                obs_swap(g, i, h).wait_send()
+
+    by_depth(parts_sent)
     forward_all(1, (ng, kk), 0).wait_send()
     sib_pert(c).wait_send()
     for way in (0, 1):

time: 40.4 us -> 39.9 us (0.988)
  Pallas kernels: 37.3 us -> 36.7 us
    pallas_call x1, Pallas kernels: 37.3 us -> 36.7 us  [shards(): pl.pallas_call(functools.partial(kernel, (nr, nd, nm, nl, mm, tt, kk)), o...]
where the time goes in v6:
time: 39.9 us; the launch traced here: 39.6 us
  Pallas kernels  36.7 us (92%)
  between operations  1.81 us (5%)
  local copies, waits for them, and re-layouts  1.08 us (3%)
    pallas_call x1, Pallas kernels, shards(): pl.pallas_call(functools.partial(kernel, (nr, nd, nm, nl, mm, tt, kk)), o...  36.7 us
    unnamed x1, local copies, waits for them, and re-layouts  1.08 us

profile of v6, /device:TPU:0, one launch (start us, length us, event | category | flops | bytes accessed | tf_op | source)
XLA Modules:
  0.0 39.6 jit_solution(12062114524166845361)
XLA Ops:
  0.6 36.7 %shard_map.77 = (bf16[7,96,1024]{2,1,0:T(8,128)(2,1)S(1)}, f32[1,1]{1,0:T(1,128)S(1)}) custom-call(f32[7]{0:T(128)} %weights_hbm.1, bf16[7,96,1024]{2,1,0:T(8,128)(2,1)} %ensemble.1, s32[1,512]{1,0:T(1,128)} %bitcast.4, f32[1,512]{1,0:T(1,128)} %bitcast.5, f32[1,512]{1,0:T(1,128)} %bitcast.6, f32[96,512]{1,0:T(8,128)} %noise.1), custom_call_target="tpu_custom_call" | custom-call | tf_op jit(solution)/shard_map/pallas_call | solution.py:809
  37.4 1.1 %copy.12 = bf16[7,96,1024]{2,1,0:T(8,128)(2,1)} copy(bf16[7,96,1024]{2,1,0:T(8,128)(2,1)S(1)} %shard_map.78) | data formatting | bytes 2752512
  (1 shorter events, 0.0 us)

commit v7 on v6

--- a/solution.py
+++ b/solution.py
@@ -50,36 +50,26 @@
     result,
     scale,
     answer,
+    plane_sent,
+    side_sent,
+    recv_pert,
     small_sem,
     local_sem,
     send_e,
     recv_e,
-    send_p,
     recv_p,
     send_q,
     recv_q,
-    send_o,
     recv_o,
     send_g,
     recv_g,
-    send_y,
     recv_y,
-    send_z,
     recv_z,
-    send_st,
-    recv_st,
     recv_pos,
-    send_ps,
-    recv_ps,
-    send_pz,
     recv_pz,
-    send_pf,
-    recv_pf,
-    send_f,
     recv_f,
     send_out,
     recv_out,
-    own_out,
 ):
     nr, nd, nm, nl, mm, tt, kk = sizes
     ng = nm // 2
@@ -220,12 +210,12 @@
 
     def part_copy(i):
         to = (d + i) % nd
-        return rdma(part, part_in.at[d], send_p.at[i - 1], recv_p.at[i - 1], dev(depth=to))
+        return rdma(part, part_in.at[d], plane_sent.at[0], recv_p.at[i - 1], dev(depth=to))
 
     def part_from(i):
         frm = (d + i) % nd
         return rdma(
-            part, part_in.at[frm], send_p.at[i - 1], recv_p.at[nd - i - 1], dev(depth=frm)
+            part, part_in.at[frm], plane_sent.at[0], recv_p.at[nd - i - 1], dev(depth=frm)
         )
 
     @pl.when(d < nd - 1)
@@ -241,7 +231,7 @@
         return rdma(
             pos.at[1],
             pos.at[2 - 2 * side],
-            send_st.at[side],
+            side_sent.at[side],
             recv_pos.at[1 - side],
             dev(region=r + (2 * side - 1)),
         )
@@ -250,7 +240,7 @@
         return rdma(
             pos.at[1],
             pos.at[2 * side],
-            send_st.at[side],
+            side_sent.at[side],
             recv_pos.at[side],
             dev(region=r + (2 * side - 1)),
         )
@@ -315,47 +305,55 @@
     def obs_copy(g, h):
         block = obs_at(me, 1, parts[h])
         return rdma(
-            block, block, send_o.at[g - 1], recv_o.at[g - 1], dev(member=(me + 2 * g) % nm)
+            block, block, plane_sent.at[0], recv_o.at[g - 1], dev(member=(me + 2 * g) % nm)
         )
 
     def obs_from(g, h):
         block = obs_at(cross(g), 1, parts[h])
-        return rdma(block, block, send_o.at[g - 1], recv_o.at[ng - g - 1], dev(member=sib))
+        return rdma(block, block, plane_sent.at[0], recv_o.at[ng - g - 1], dev(member=sib))
 
     def obs_swap(g, i, h):
         block = obs_at(cross(g), 1, parts[h])
         return rdma(
-            block, block, send_y.at[g - 1, i - 1], recv_y.at[g - 1, i - 1], dev(depth=(d + i) % nd)
+            block, block, plane_sent.at[0], recv_y.at[g - 1, i - 1], dev(depth=(d + i) % nd)
         )
 
     def swap_from(g, i, h):
         block = obs_at(cross(g), 1, parts[h])
         return rdma(
-            block, block, send_y.at[g - 1, i - 1], recv_y.at[g - 1, nd - i - 1], dev(depth=h)
+            block, block, plane_sent.at[0], recv_y.at[g - 1, nd - i - 1], dev(depth=h)
         )
 
     def side_obs(side, slot, extent):
         return rdma(
             obs_at(slot, 1, extent),
             obs_at(slot, 2 if side == 0 else 0, extent),
-            send_z.at[side],
+            side_sent.at[side],
             recv_z.at[1 - side],
             dev(region=r + (2 * side - 1)),
         )
 
-    def side_all(side):
-        block = obs.at[pl.ds(0, ng), :, pl.ds(kk, kk)]
-        return rdma(
-            block, block, send_z.at[side], recv_z.at[side], dev(region=r + (2 * side - 1))
-        )
+    slot_bytes = mm * kk * 2
+    stat_bytes = 8 * kk * 4
+
+    def group(size):
+        block = taper.at[pl.ds(0, size // (4 * half))]
+        return rdma(block, block, plane_sent.at[0], recv_pert.at[0], dev(member=sib))
+
+    def group_from(size, number):
+        block = taper.at[pl.ds(0, size // (4 * half))]
+        return rdma(block, block, side_sent.at[number], recv_z.at[number], dev(member=sib))
+
+    def sent_of(w):
+        return plane_sent.at[0] if w == 1 else side_sent.at[w // 2]
 
     def obs_forward(w, slot, extent, number):
         block = obs_at(slot, w, extent)
-        return rdma(block, block, send_f.at[w], recv_f.at[number], dev(member=sib))
+        return rdma(block, block, sent_of(w), recv_f.at[number], dev(member=sib))
 
     def forward_all(w, wide, number):
         block = obs.at[pl.ds(0, wide[0]), :, pl.ds(0, wide[1])]
-        return rdma(block, block, send_f.at[w], recv_f.at[number], dev(member=sib))
+        return rdma(block, block, sent_of(w), recv_f.at[number], dev(member=sib))
 
     def cross(g):
         return 2 * ((q + g) % ng) + c
@@ -399,8 +397,8 @@
         return rdma(
             stats.at[1],
             stats.at[2 - 2 * side],
-            send_st.at[side],
-            recv_st.at[1 - side],
+            side_sent.at[side],
+            recv_z.at[1 - side],
             dev(region=r + (2 * side - 1)),
         )
 
@@ -526,21 +524,21 @@
 
     def sib_pert(slot):
         block = pert.at[slot, :, pl.ds(kk, kk)]
-        return rdma(block, block, send_ps.at[0], recv_ps.at[0], dev(member=sib))
+        return rdma(block, block, plane_sent.at[0], recv_pert.at[0], dev(member=sib))
 
     def side_pert(side):
         window = 2 * kk if side == 0 else 0
         return rdma(
             pert.at[c, :, pl.ds(kk, kk)],
             pert.at[c, :, pl.ds(window, kk)],
-            send_pz.at[side],
+            side_sent.at[side],
             recv_pz.at[1 - side],
             dev(region=r + (2 * side - 1)),
         )
 
     def pert_forward(side, slot):
         block = pert.at[slot, :, pl.ds(2 * kk * side, kk)]
-        return rdma(block, block, send_pf.at[side], recv_pf.at[side], dev(member=sib))
+        return rdma(block, block, side_sent.at[side], recv_pert.at[0], dev(member=sib))
 
     def make_pert():
         everyone = jnp.where(trow < r, tot_in[0], jnp.where(trow > r, tot_in[1], own_total))
@@ -623,7 +621,7 @@
 
         @pl.when(has_side[side])
         def _():
-            side_all(side).wait_recv()
+            group_from(ng * slot_bytes + stat_bytes, side).wait_recv()
             for g in range(ng):
                 obs_forward(2 * side, cross(g), whole_slot, nd + side).start()
 
@@ -642,13 +640,6 @@
 
         @pl.when(has_side[side])
         def _():
-            rdma(
-                stats.at[1],
-                stats.at[2 * side],
-                send_st.at[side],
-                recv_st.at[side],
-                dev(region=r + (2 * side - 1)),
-            ).wait_recv()
             forward_all(2 * side, (ng, kk), nd + side).wait_recv()
 
             transpose_part(2 * side, whole_slot)
@@ -667,7 +658,7 @@
             dev(member=sib),
         )
         here = pltpu.make_async_copy(
-            result.at[l, c, :, cols], out_block(l, c, columns), own_out.at[0]
+            result.at[l, c, :, cols], out_block(l, c, columns), local_sem.at[0]
         )
         return there, here
 
@@ -718,12 +709,13 @@
         return carry
 
     lax.fori_loop(3, ready, ahead, 0)
-    sib_pert(1 - c).wait_recv()
-    for side in (0, 1):
-
-        @pl.when(has_side[side])
-        def _():
-            pert_forward(side, 1 - c).wait_recv()
+    @pl.when(middle)
+    def _():
+        group(3 * slot_bytes).wait_recv()
+
+    @pl.when(jnp.logical_not(middle))
+    def _():
+        group(2 * slot_bytes).wait_recv()
 
     def late_variable(l, carry):
         by_place(lambda sides: finish_variable(l, sides))
@@ -754,22 +746,21 @@
     rdma(sent, sent, send_e.at[0], recv_e.at[0], dev(member=sib)).wait_send()
     mine = out.at[:, :, pl.ds(pl.multiple_of(c * half, 128), half)]
     other = out.at[:, :, pl.ds(pl.multiple_of((1 - c) * half, 128), half)]
-    pltpu.make_async_copy(mine, mine, own_out.at[0]).wait()
+    pltpu.make_async_copy(mine, mine, local_sem.at[0]).wait()
     theirs = rdma(other, other, send_out.at[0], recv_out.at[0], dev(member=sib))
     theirs.wait_send()
     theirs.wait_recv()
-    for i in range(1, nd):
-        part_copy(i).wait_send()
     square_all.wait_send()
-    def parts_sent(h):
-        for g in range(1, ng):
-            obs_copy(g, h).wait_send()
-            for i in range(1, nd):
-                obs_swap(g, i, h).wait_send()
-
-    by_depth(parts_sent)
-    forward_all(1, (ng, kk), 0).wait_send()
-    sib_pert(c).wait_send()
+
+    def plane_done(h):
+        part_bytes = mm * parts[h][1] * 2
+        group(
+            (nd - 1) * (mm + 16) * kk * 2
+            + (ng + 1) * slot_bytes
+            + (ng - 1) * nd * part_bytes
+        ).wait_send()
+
+    by_depth(plane_done)
     for way in (0, 1):
 
         @pl.when(has_side[1 - way])
@@ -780,14 +771,7 @@
 
         @pl.when(has_side[side])
         def _():
-            side_all(side).wait_send()
-            forward_all(2 * side, (ng, kk), nd + side).wait_send()
-            side_pert(side).wait_send()
-            pert_forward(side, c).wait_send()
-            both = stats.at[pl.ds(0, 2)]
-            rdma(
-                both, both, send_st.at[side], recv_st.at[side], dev(region=r + (2 * side - 1))
-            ).wait_send()
+            group_from((2 * ng + 2) * slot_bytes + 2 * stat_bytes, side).wait_send()
 
 
 def hand_on(block, out):
@@ -839,34 +823,24 @@
                 pltpu.VMEM((nl, 2, mm, half), BF16),
                 pltpu.VMEM((1, 128), F32),
                 pltpu.SemaphoreType.REGULAR((2,)),
+                dma((1,)),
+                dma((2,)),
+                dma((1,)),
                 dma((4,)),
                 dma((3,)),
                 dma((1,)),
                 dma((nl - 1 + PIECES,)),
                 dma((nd - 1,)),
-                dma((nd - 1,)),
                 dma((1,)),
                 dma((1,)),
-                dma((ng - 1,)),
                 dma((ng - 1,)),
                 dma((2,)),
                 dma((2,)),
                 dma((ng - 1, nd - 1)),
-                dma((ng - 1, nd - 1)),
                 dma((2,)),
                 dma((2,)),
                 dma((2,)),
-                dma((2,)),
-                dma((2,)),
-                dma((1,)),
-                dma((1,)),
-                dma((2,)),
-                dma((2,)),
-                dma((2,)),
-                dma((2,)),
-                dma((3,)),
                 dma((nd + 2,)),
-                dma((1,)),
                 dma((1,)),
                 dma((1,)),
             ],

time: 39.9 us -> 39.7 us (level)
  no operation moved by 1% of the time
where the time goes in v7:
time: 39.7 us; the launch traced here: 39.4 us
  Pallas kernels  36.6 us (92%)
  between operations  1.81 us (5%)
  local copies, waits for them, and re-layouts  1.08 us (3%)
    pallas_call x1, Pallas kernels, shards(): pl.pallas_call(functools.partial(kernel, (nr, nd, nm, nl, mm, tt, kk)), o...  36.6 us
    unnamed x1, local copies, waits for them, and re-layouts  1.08 us

profile of v7, /device:TPU:0, one launch (start us, length us, event | category | flops | bytes accessed | tf_op | source)
XLA Modules:
  0.0 39.4 jit_solution(4099880328574525945)
XLA Ops:
  0.6 36.6 %shard_map.77 = (bf16[7,96,1024]{2,1,0:T(8,128)(2,1)S(1)}, f32[1,1]{1,0:T(1,128)S(1)}) custom-call(f32[7]{0:T(128)} %weights_hbm.1, bf16[7,96,1024]{2,1,0:T(8,128)(2,1)} %ensemble.1, s32[1,512]{1,0:T(1,128)} %bitcast.4, f32[1,512]{1,0:T(1,128)} %bitcast.5, f32[1,512]{1,0:T(1,128)} %bitcast.6, f32[96,512]{1,0:T(8,128)} %noise.1), custom_call_target="tpu_custom_call" | custom-call | tf_op jit(solution)/shard_map/pallas_call | solution.py:793
  37.2 1.1 %copy.12 = bf16[7,96,1024]{2,1,0:T(8,128)(2,1)} copy(bf16[7,96,1024]{2,1,0:T(8,128)(2,1)S(1)} %shard_map.78) | data formatting | bytes 2752512
  (1 shorter events, 0.0 us)

commit v8 on v7

--- a/solution.py
+++ b/solution.py
@@ -287,41 +287,47 @@
     square_rest = squares.at[pl.ds(0, nm - 1)]
     square_all = rdma(square_rest, square_rest, send_q.at[0], recv_q.at[0], dev(member=sib))
 
-    first_part = kk // (2 * nd)
-    cuts = [0] + [first_part + (kk - first_part) * h // (nd - 1) for h in range(nd)]
-    parts = [(cuts[h], cuts[h + 1] - cuts[h]) for h in range(nd)]
+    def cuts(first):
+        at = [0] + [first + (kk - first) * h // (nd - 1) for h in range(nd)]
+        return [(at[h], at[h + 1] - at[h]) for h in range(nd)]
+
+    shares = (cuts(kk // nd), cuts(kk // (2 * nd)))
     whole_slot = (0, kk)
-
-    def by_depth(step, ahead=0):
+    first_region = jnp.logical_and(r == 0, ng == 2)
+    sends_late = jnp.logical_and(first_region, q == 1)
+    takes_late = jnp.logical_and(first_region, q == 0)
+
+    def by_depth(step, ahead=0, late=takes_late):
         for h in range(nd):
-
-            @pl.when(d == (h - ahead) % nd)
-            def _():
-                step(h)
+            for parts, chosen in zip(shares, (jnp.logical_not(late), late)):
+
+                @pl.when(jnp.logical_and(d == (h - ahead) % nd, chosen))
+                def _():
+                    step(parts[h])
 
     def obs_at(slot, w, extent):
         return obs.at[slot, :, pl.ds(w * kk + extent[0], extent[1])]
 
-    def obs_copy(g, h):
-        block = obs_at(me, 1, parts[h])
+    def obs_copy(g, extent):
+        block = obs_at(me, 1, extent)
         return rdma(
             block, block, plane_sent.at[0], recv_o.at[g - 1], dev(member=(me + 2 * g) % nm)
         )
 
-    def obs_from(g, h):
-        block = obs_at(cross(g), 1, parts[h])
+    def obs_from(g, extent):
+        block = obs_at(cross(g), 1, extent)
         return rdma(block, block, plane_sent.at[0], recv_o.at[ng - g - 1], dev(member=sib))
 
-    def obs_swap(g, i, h):
-        block = obs_at(cross(g), 1, parts[h])
+    def obs_swap(g, i, extent):
+        block = obs_at(cross(g), 1, extent)
         return rdma(
             block, block, plane_sent.at[0], recv_y.at[g - 1, i - 1], dev(depth=(d + i) % nd)
         )
 
-    def swap_from(g, i, h):
-        block = obs_at(cross(g), 1, parts[h])
-        return rdma(
-            block, block, plane_sent.at[0], recv_y.at[g - 1, nd - i - 1], dev(depth=h)
+    def swap_from(g, i, extent):
+        block = obs_at(cross(g), 1, extent)
+        return rdma(
+            block, block, plane_sent.at[0], recv_y.at[g - 1, nd - i - 1], dev(depth=(d + i) % nd)
         )
 
     def side_obs(side, slot, extent):
@@ -337,11 +343,11 @@
     stat_bytes = 8 * kk * 4
 
     def group(size):
-        block = taper.at[pl.ds(0, size // (4 * half))]
+        block = taper.at[pl.ds(0, size // (4 * piece)), pl.ds(0, piece)]
         return rdma(block, block, plane_sent.at[0], recv_pert.at[0], dev(member=sib))
 
     def group_from(size, number):
-        block = taper.at[pl.ds(0, size // (4 * half))]
+        block = taper.at[pl.ds(0, size // (4 * piece)), pl.ds(0, piece)]
         return rdma(block, block, side_sent.at[number], recv_z.at[number], dev(member=sib))
 
     def sent_of(w):
@@ -360,7 +366,9 @@
 
     for j in range(1, nm):
         square_copy(j).start()
-    by_depth(lambda h: [obs_copy(g, h).start() for g in range(1, ng)])
+    by_depth(
+        lambda extent: [obs_copy(g, extent).start() for g in range(1, ng)], late=sends_late
+    )
     obs_forward(1, me, whole_slot, 0).start()
     send_bulk(units[LEAD:])
     for side in (0, 1):
@@ -451,21 +459,21 @@
         def _():
             stat_copy(side).start()
 
-    def hand_part(g, i, h):
+    def hand_part(g, i, extent):
         for side in (0, 1):
 
             @pl.when(has_side[side])
             def _():
-                side_obs(side, cross(g), parts[h]).start()
-
-        obs_forward(1, cross(g), parts[h], i).start()
-
-    def take_part(h):
+                side_obs(side, cross(g), extent).start()
+
+        obs_forward(1, cross(g), extent, i).start()
+
+    def take_part(extent):
         for g in range(1, ng):
-            obs_from(g, h).wait_recv()
+            obs_from(g, extent).wait_recv()
             for i in range(1, nd):
-                obs_swap(g, i, h).start()
-            hand_part(g, 0, h)
+                obs_swap(g, i, extent).start()
+            hand_part(g, 0, extent)
 
     by_depth(take_part)
 
@@ -501,8 +509,8 @@
             cov = jnp.dot(obs_t[span(w)], right, preferred_element_type=F32)
             gain[l, span(w), cols] = (cov * taper[span(w), cols]).astype(BF16)
 
-    def gain_part(l, h):
-        at = pl.ds(kk + parts[h][0], parts[h][1])
+    def gain_part(l, extent):
+        at = pl.ds(kk + extent[0], extent[1])
         cov = jnp.dot(
             obs_t[at], anom[l].reshape(members, half), preferred_element_type=F32
         )
@@ -578,23 +586,23 @@
     wait_variable(0)
     center(0)
 
-    def own_part(h):
-        forward_all(1, (1, kk + (ng - 1) * parts[h][1]), 0).wait_recv()
-        transpose_part(1, parts[h])
-        gain_part(0, h)
+    def own_part(extent):
+        forward_all(1, (1, kk + (ng - 1) * extent[1]), 0).wait_recv()
+        transpose_part(1, extent)
+        gain_part(0, extent)
 
     by_depth(own_part)
 
-    def swap_part(i, h):
+    def swap_part(i, extent):
         for g in range(1, ng):
-            swap_from(g, i, h).wait_recv()
-            hand_part(g, i, h)
+            swap_from(g, i, extent).wait_recv()
+            hand_part(g, i, extent)
 
     for i in range(1, nd):
         by_depth(functools.partial(swap_part, i), i)
     wait_variable(1)
     center(1)
-    by_depth(lambda h: gain_part(1, h))
+    by_depth(lambda extent: gain_part(1, extent))
 
     @pl.when(mid_low)
     def _():
@@ -606,11 +614,11 @@
         relay(0)
         make_pert()
 
-    def other_part(i, h):
-        forward_all(1, (1, (ng - 1) * parts[h][1]), i).wait_recv()
-        transpose_part(1, parts[h])
-        gain_part(0, h)
-        gain_part(1, h)
+    def other_part(i, extent):
+        forward_all(1, (1, (ng - 1) * extent[1]), i).wait_recv()
+        transpose_part(1, extent)
+        gain_part(0, extent)
+        gain_part(1, extent)
 
     for i in range(1, nd):
         by_depth(functools.partial(other_part, i), i)
@@ -752,15 +760,17 @@
     theirs.wait_recv()
     square_all.wait_send()
 
-    def plane_done(h):
-        part_bytes = mm * parts[h][1] * 2
+    def plane_done(sent, taken):
+        columns = sent[1] + (nd - 1) * taken[1]
         group(
             (nd - 1) * (mm + 16) * kk * 2
             + (ng + 1) * slot_bytes
-            + (ng - 1) * nd * part_bytes
+            + (ng - 1) * mm * columns * 2
         ).wait_send()
 
-    by_depth(plane_done)
+    by_depth(
+        lambda sent: by_depth(lambda taken: plane_done(sent, taken)), late=sends_late
+    )
     for way in (0, 1):
 
         @pl.when(has_side[1 - way])

time: 39.7 us -> 39.7 us (level)
  no operation moved by 1% of the time
where the time goes in v8:
time: 39.7 us; the launch traced here: 39.4 us
  Pallas kernels  36.6 us (92%)
  between operations  1.81 us (5%)
  local copies, waits for them, and re-layouts  1.08 us (3%)
    pallas_call x1, Pallas kernels, shards(): pl.pallas_call(functools.partial(kernel, (nr, nd, nm, nl, mm, tt, kk)), o...  36.6 us
    unnamed x1, local copies, waits for them, and re-layouts  1.08 us

profile of v8, /device:TPU:0, one launch (start us, length us, event | category | flops | bytes accessed | tf_op | source)
XLA Modules:
  0.0 39.4 jit_solution(11241729366716604828)
XLA Ops:
  0.6 36.6 %shard_map.77 = (bf16[7,96,1024]{2,1,0:T(8,128)(2,1)S(1)}, f32[1,1]{1,0:T(1,128)S(1)}) custom-call(f32[7]{0:T(128)} %weights_hbm.1, bf16[7,96,1024]{2,1,0:T(8,128)(2,1)} %ensemble.1, s32[1,512]{1,0:T(1,128)} %bitcast.4, f32[1,512]{1,0:T(1,128)} %bitcast.5, f32[1,512]{1,0:T(1,128)} %bitcast.6, f32[96,512]{1,0:T(8,128)} %noise.1), custom_call_target="tpu_custom_call" | custom-call | tf_op jit(solution)/shard_map/pallas_call | solution.py:803
  37.2 1.1 %copy.12 = bf16[7,96,1024]{2,1,0:T(8,128)(2,1)} copy(bf16[7,96,1024]{2,1,0:T(8,128)(2,1)S(1)} %shard_map.78) | data formatting | bytes 2752512
  (1 shorter events, 0.0 us)

commit v9 on v8

--- a/solution.py
+++ b/solution.py
@@ -275,17 +275,13 @@
     squares[me] = jnp.where(qrow == 0, own_sum, own_square)
     obs[me, :, kk : 2 * kk] = spread_in.astype(BF16)
 
-    def square_copy(j):
-        return rdma(
-            squares.at[me],
-            squares.at[me],
-            send_q.at[0],
-            recv_q.at[0],
-            dev(member=(me + j) % nm),
-        )
-
-    square_rest = squares.at[pl.ds(0, nm - 1)]
-    square_all = rdma(square_rest, square_rest, send_q.at[0], recv_q.at[0], dev(member=sib))
+    def square_copy(slot, to, number):
+        block = squares.at[slot]
+        return rdma(block, block, send_q.at[0], recv_q.at[number], dev(member=to))
+
+    def square_wait(count, number):
+        block = squares.at[pl.ds(0, count)]
+        return rdma(block, block, send_q.at[0], recv_q.at[number], dev(member=sib))
 
     def cuts(first):
         at = [0] + [first + (kk - first) * h // (nd - 1) for h in range(nd)]
@@ -364,8 +360,9 @@
     def cross(g):
         return 2 * ((q + g) % ng) + c
 
-    for j in range(1, nm):
-        square_copy(j).start()
+    for g in range(1, ng):
+        square_copy(me, (me + 2 * g) % nm, 1).start()
+    square_copy(me, sib, 0).start()
     by_depth(
         lambda extent: [obs_copy(g, extent).start() for g in range(1, ng)], late=sends_late
     )
@@ -379,7 +376,10 @@
             pos_from(side).wait_recv()
             make_taper(2 * side)
 
-    square_all.wait_recv()
+    square_wait(ng - 1, 1).wait_recv()
+    for g in range(1, ng):
+        square_copy(cross(g), sib, 0).start()
+    square_wait(ng, 0).wait_recv()
     moments = [squares[j] for j in range(nm)]
     obs_mean = sum(m[0:1] for m in moments) / members
     deviation = predicted - obs_mean
@@ -758,7 +758,7 @@
     theirs = rdma(other, other, send_out.at[0], recv_out.at[0], dev(member=sib))
     theirs.wait_send()
     theirs.wait_recv()
-    square_all.wait_send()
+    square_wait(nm - 1, 0).wait_send()
 
     def plane_done(sent, taken):
         columns = sent[1] + (nd - 1) * taken[1]
@@ -842,7 +842,7 @@
                 dma((nl - 1 + PIECES,)),
                 dma((nd - 1,)),
                 dma((1,)),
-                dma((1,)),
+                dma((2,)),
                 dma((ng - 1,)),
                 dma((2,)),
                 dma((2,)),

time: 39.7 us -> 39.6 us (level)
  no operation moved by 1% of the time
where the time goes in v9:
time: 39.6 us; the launch traced here: 39.4 us
  Pallas kernels  36.5 us (92%)
  between operations  1.81 us (5%)
  local copies, waits for them, and re-layouts  1.08 us (3%)
    pallas_call x1, Pallas kernels, shards(): pl.pallas_call(functools.partial(kernel, (nr, nd, nm, nl, mm, tt, kk)), o...  36.5 us
    unnamed x1, local copies, waits for them, and re-layouts  1.08 us

profile of v9, /device:TPU:0, one launch (start us, length us, event | category | flops | bytes accessed | tf_op | source)
XLA Modules:
  0.0 39.4 jit_solution(1154234751835754240)
XLA Ops:
  0.6 36.5 %shard_map.77 = (bf16[7,96,1024]{2,1,0:T(8,128)(2,1)S(1)}, f32[1,1]{1,0:T(1,128)S(1)}) custom-call(f32[7]{0:T(128)} %weights_hbm.1, bf16[7,96,1024]{2,1,0:T(8,128)(2,1)} %ensemble.1, s32[1,512]{1,0:T(1,128)} %bitcast.4, f32[1,512]{1,0:T(1,128)} %bitcast.5, f32[1,512]{1,0:T(1,128)} %bitcast.6, f32[96,512]{1,0:T(8,128)} %noise.1), custom_call_target="tpu_custom_call" | custom-call | tf_op jit(solution)/shard_map/pallas_call | solution.py:803
  37.2 1.1 %copy.12 = bf16[7,96,1024]{2,1,0:T(8,128)(2,1)} copy(bf16[7,96,1024]{2,1,0:T(8,128)(2,1)S(1)} %shard_map.78) | data formatting | bytes 2752512
  (1 shorter events, 0.0 us)
